TPU v7x, 256 devices: a whole 4x4x8 slice. The times are simulated.
256 devices in a mesh: prow: 8 (over z), pcol: 32 (over y, x, core).
Axes of the slice: x: 4, y: 4, z: 8, core: 2. Of those that a mesh axis runs over, the one named last changes fastest.
Arguments:
- points: float32 [1, 32, 2, 1024], P(None, 'pcol'), may hold values from 0 to 1
- range_length: float32 [1], replicated, may hold values from 0.05 to 0.15
- smoothness: int32 [1], replicated, may hold values from 0 to 2
- sketch_bank: bfloat16 [32, 48, 1024], P('pcol'), may hold values from -6 to 6
- sketch_ids: int32 [4, 8, 1, 32], P(None, 'prow', None, 'pcol'), may hold values from 0 to 31
- tile_ranks: int32 [4, 8, 1, 32], P(None, 'prow', None, 'pcol'), may hold values from 16 to 48
Outputs:
- y_factors: float32 [4, 8, 1, 32, 48, 1024], P(None, 'prow', None, 'pcol')
- c_factors: float32 [4, 8, 1, 32, 48, 1024], P(None, 'prow', None, 'pcol')
- tile_error: float32 [4, 8, 1, 32], P(None, 'prow', None, 'pcol')
- rank_total: int32 [1], replicated
All inputs are finite; a program needn't handle non-finite values.
Results may differ from a plain program's by a relative error of at most 0.0098.
The roundings to bfloat16 on the way count: a program that leaves them out, or rounds other values in their place, can miss the bound.
Values may be sent and summed in bfloat16 or wider, within the bound.
No kernel may reach another device: no remote copies, remote signals or barrier semaphores. Data moves between devices by JAX's collectives and lax.ppermute only.
A program may use at most 64 MiB of HBM per device.

v0:
```python
import jax
import jax.numpy as jnp
from jax import lax
from jax.sharding import Mesh
from jax.sharding import PartitionSpec as P

PCOL = ("pcol_0", "pcol_1", "pcol_2")
PROW_PCOL = ("prow", "pcol_0", "pcol_1", "pcol_2")


def joined_along(parts, dim):
    shape = list(parts.shape[1:])
    shape[dim] *= parts.shape[0]
    return jnp.moveaxis(parts, 0, dim).reshape(shape)


def sent_to_all(x, axis):
    copies = jnp.broadcast_to(x, (lax.axis_size(axis), *x.shape))
    return lax.all_to_all(copies, axis, split_axis=0, concat_axis=0, tiled=True)


def collect(x, axis, dim):
    return joined_along(sent_to_all(x, axis), dim)


def one_axis_at_a_time(x, axes):
    for axis in axes:
        x = lax.psum(x, axis)
    return x


def kernel_factors(smoothness, range_length):
    morton_value = smoothness[0].astype(jnp.float32)
    kernel_scale = jnp.sqrt(2.0 * morton_value + 1.0) / range_length[0]
    linear_factor = jnp.where(smoothness[0] >= 1, 1.0, 0.0).astype(jnp.float32)
    squared_distance = jnp.where(smoothness[0] >= 2, 1.0 / 3.0, 0.0).astype(jnp.float32)
    return (kernel_scale, linear_factor, squared_distance)


def covariance_tile(row_locations, column_locations, kernel_scale, linear_factor, squared_distance):
    offset_horizontal = row_locations[0][:, None] - column_locations[0][None, :]
    offset_vertical = row_locations[1][:, None] - column_locations[1][None, :]
    scaled_distance = kernel_scale * jnp.sqrt(
        offset_horizontal * offset_horizontal + offset_vertical * offset_vertical
    )
    return (
        1.0 + linear_factor * scaled_distance + squared_distance * scaled_distance * scaled_distance
    ) * jnp.exp(-scaled_distance)


def compress(tile_low, sketch, rank):
    keep = jnp.arange(sketch.shape[0]) < rank
    sketch = jnp.where(keep[:, None], sketch, jnp.zeros_like(sketch))
    sketched = lax.dot_general(
        sketch, tile_low, (((1,), (1,)), ((), ())), preferred_element_type=jnp.float32
    )
    product = jnp.dot(sketched.astype(jnp.bfloat16), tile_low, preferred_element_type=jnp.float32)
    gram = jnp.dot(sketched, sketched.T, precision=lax.Precision.HIGHEST)
    shift = 0.1 * jnp.trace(gram) / rank.astype(jnp.float32)
    gram = gram + jnp.diag(jnp.where(keep, shift, jnp.ones_like(shift)))
    factor = jnp.linalg.cholesky(gram)
    coeffs = jax.scipy.linalg.cho_solve((factor, True), product)
    approx = lax.dot_general(
        sketched, coeffs, (((0,), (0,)), ((), ())), precision=lax.Precision.HIGHEST
    )
    error = tile_low.astype(jnp.float32) - approx
    return (sketched, coeffs, jnp.sum(error * error))


def per_device(points, range_length, smoothness, sketch_bank, sketch_ids, tile_ranks):
    row_count = lax.axis_size("prow")
    col_count = lax.axis_size(PCOL)
    row_place = lax.axis_index("prow")
    col_place = lax.axis_index(PCOL)
    row_tiles = sketch_ids.shape[0]
    col_tiles = sketch_ids.shape[2]
    tile_size = points.shape[3]
    sketch_rows = sketch_bank.shape[1]
    slots_total = row_tiles * col_tiles
    tiles_across = col_tiles * col_count
    kernel_scale, linear_factor, squared_distance = kernel_factors(smoothness, range_length)
    gathered = collect(points, PCOL, 1)
    every_block = gathered.reshape(tiles_across, 2, tile_size)
    row_index = jnp.arange(row_tiles, dtype=jnp.int32) * row_count + row_place
    col_index = jnp.arange(col_tiles, dtype=jnp.int32) * col_count + col_place
    slot_row = jnp.repeat(row_index, col_tiles)
    slot_col = jnp.tile(col_index, row_tiles)
    own_ids = sketch_ids.reshape(slots_total)
    own_ranks = tile_ranks.reshape(slots_total)
    lower = slot_col <= slot_row
    offdiag = slot_col < slot_row
    ranks_local = jnp.sum(jnp.where(offdiag, own_ranks, 0))
    rank_sum = one_axis_at_a_time(ranks_local, PROW_PCOL)
    bank_whole = lax.all_gather(sketch_bank, PCOL, axis=0, tiled=True)
    chosen = bank_whole[own_ids]
    row_points_all = every_block[slot_row]
    col_points_all = every_block[slot_col]

    def one_tile(row_locations, column_locations, sketch, rank):
        tile_block = covariance_tile(
            row_locations, column_locations, kernel_scale, linear_factor, squared_distance
        )
        norm_sq = jnp.sum(tile_block * tile_block)
        sketched, coeffs, err_sq = compress(tile_block.astype(jnp.bfloat16), sketch, rank)
        return (sketched, coeffs, norm_sq, err_sq)

    def mapped(inputs):
        return one_tile(inputs[0], inputs[1], inputs[2], inputs[3])

    sketched_all, coeffs_all, norm_all, err_all = lax.map(
        mapped, (row_points_all, col_points_all, chosen, own_ranks)
    )
    norm_local = jnp.sum(jnp.where(lower, jnp.where(offdiag, 2.0, 1.0) * norm_all, 0.0))
    total = one_axis_at_a_time(norm_local, PROW_PCOL)
    errors = (
        jnp.where(offdiag, jnp.sqrt(err_all), jnp.sqrt(norm_all)) * tiles_across / jnp.sqrt(total)
    )
    errors = jnp.where(lower, errors, 0.0)
    out_shape = (row_tiles, 1, col_tiles, 1, sketch_rows, tile_size)
    y_out = jnp.where(offdiag[:, None, None], sketched_all, 0.0).reshape(out_shape)
    c_out = jnp.where(offdiag[:, None, None], coeffs_all, 0.0).reshape(out_shape)
    err_out = errors.reshape(row_tiles, 1, col_tiles, 1)
    rank_out = rank_sum.reshape(1)
    return (y_out, c_out, err_out, rank_out)


def solution(mesh):
    split = Mesh(
        mesh.devices.reshape(mesh.shape["prow"], 4, 4, 2), ("prow", "pcol_0", "pcol_1", "pcol_2")
    )
    placed = (
        P(None, PCOL, None, None),
        P(),
        P(),
        P(PCOL, None, None),
        P(None, "prow", None, PCOL),
        P(None, "prow", None, PCOL),
    )
    return jax.shard_map(
        per_device,
        mesh=split,
        in_specs=placed,
        out_specs=(
            P(None, "prow", None, PCOL, None, None),
            P(None, "prow", None, PCOL, None, None),
            P(None, "prow", None, PCOL),
            P(),
        ),
        check_vma=False,
    )
```

profile of v0, /device:TPU:1, one launch (start us, length us, event | category | flops | bytes accessed | tf_op | source)
XLA Modules:
  0.0 285.3 jit_solution(14311572031564186619)
XLA Ops:
  7.2 0.7 all-gather.2.cloned.1.call-update
  7.9 1.5 broadcast_in_dim.93
  9.4 8.6 %all-to-all-start = ((f32[32,1,1,2,1024]{4,3,2,1,0:T(2,128)}), f32[32,1,1,2,1024]{4,3,2,1,0:T(2,128)S(1)}, u32[]{:S(2)}, u32[]{:S(2)}) async-start(f32[32,1,1,2,1024]{4,3,2,1,0:T(2,128)} %broadcast_in_dim.93), calls=%async_computation | async-start | bytes 524288 | tf_op jit(solution)/shard_map/all_to_all | solution.py:19
  18.0 0.7 fusion.23
  20.1 1.3 select_reduce_fusion.2
  21.4 5.4 %all-to-all-done = f32[32,1,1,2,1024]{4,3,2,1,0:T(2,128)S(1)} async-done(((f32[32,1,1,2,1024]{4,3,2,1,0:T(2,128)}), f32[32,1,1,2,1024]{4,3,2,1,0:T(2,128)S(1)}, u32[]{:S(2)}, u32[]{:S(2)}) %all-to-all-start) | async-done | bytes 262176 | tf_op jit(solution)/shard_map/all_to_all | solution.py:19
  28.0 36.6 %all-gather.2.cloned.1.call-done = bf16[32,48,1024]{2,1,0:T(8,128)(2,1)} async-done(((bf16[1,48,1024]{2,1,0:T(8,128)(2,1)}), bf16[32,48,1024]{2,1,0:T(8,128)(2,1)}) %all-gather.2.cloned.1.call-update) | async-done | bytes 3145744 | tf_op jit(solution)/shard_map/all_gather | solution.py:94
  64.6 2.5 gather_fusion
  67.2 136.1 %while.17 = (s32[]{:T(128)}, f32[4,48,1024]{2,1,0:T(8,128)S(1)}, f32[4,48,1024]{2,1,0:T(8,128)S(1)}, f32[4]{0:T(128)S(1)}, f32[4]{0:T(128)S(1)}, /*index=5*/s32[...) while((s32[]{:T(128)}, f32[4,48,1024]{2,1,0:T(8,128)S(1)}, ...), condition=%wide.region_6.7_spmd.clone, body=%wide.region_0.6_spmd.sunk.clone | while | flops 954344128 | bytes 2675283 | solution.py:110
  68.5 0.7 iota_compare_fusion.6
  69.2 4.2 %multiply_reduce_fusion.6 = f32[]{:T(128)} fusion(f32[]{:T(128)} %get-tuple-element.278, f32[1024]{0:T(1024)S(1)} %bitcast.123, f32[1024]{0:T(1024)S(1)} %bitcast.127, f32[1024]{0:T(1024)S(1)} %bitcast.119, f32[1024]{0:T(1024)S(1)} %bitcast.131, f32[]{:T(128)} %get-tuple-element.275, f32[]{:T(128)} %get-tuple-element.274), kind=kLoop, calls=%fused_computation.7.clone.1.clone | loop fusion | flops 15728639 | bytes 16400 | tf_op jit(solution)/shard_map/while/body/eval_jaxpr/reduce_sum | solution.py:103
  73.4 0.8 dynamic_update_slice.26
  74.2 3.1 %bitcast_dynamic-update-slice_fusion.6 = (f32[4,48,1024]{2,1,0:T(8,128)S(1)}, f32[48,1024]{1,0:T(8,128)S(1)}) fusion(f32[4,48,1024]{2,1,0:T(8,128)S(1)} %get-tuple-element.256, s32[]{:T(128)S(6)} %copy.24, f32[]{:T(128)} %get-tuple-element.278, f32[1024]{0:T(1024)S(1)} %bitcast.124, f32[1024]{0:T(1024)S(1)} %bitcast.128, ...), kind=kOutput, calls=%fused_computation.12.clone.1.clone | convolution fusion | flops 115392512 | bytes 509452 | tf_op jit(solution)/shard_map/while/body/eval_jaxpr/dot_general | solution.py:54
  77.4 1.0 select_reduce_fusion.7
  79.1 0.7 broadcast_select_fusion.3
  79.9 4.4 %cholesky.73 = f32[48,48]{1,0:T(8,128)S(1)} custom-call(f32[48,48]{1,0:T(8,128)S(1)} %fusion.68), custom_call_target="Cholesky" | custom-call | tf_op jit(solution)/shard_map/while/body/eval_jaxpr/jit(cholesky)/cholesky | solution.py:61
  85.0 0.7 fusion.69
  85.6 3.7 %custom-call.20 = f32[1,48,48]{1,2,0:T(8,128)S(1)} custom-call(f32[1,48,48]{2,1,0:T(8,128)S(1)} %fusion.69), custom_call_target="InvertDiagBlocksLowerTriangular" | custom-call | tf_op jit(solution)/shard_map/while/body/eval_jaxpr/jit(_cho_solve)/triangular_solve | solution.py:62
  89.3 3.2 %fusion.67 = f32[48,1024]{1,0:T(8,128)S(1)} fusion(f32[]{:T(128)} %get-tuple-element.278, f32[1024]{0:T(1024)S(1)} %bitcast.125, f32[1024]{0:T(1024)S(1)} %bitcast.129, f32[1024]{0:T(1024)S(1)} %bitcast.121, f32[1024]{0:T(1024)S(1)} %bitcast.133, f32[]{:T(128)} %get-tuple-element.275, f32[]{:T(128)} %get-tuple-element.274, ...), kind=kOutput, calls=%fused_computation.9.clone.1.clone | convolution fusion | flops 115392512 | bytes 409612 | tf_op jit(solution)/shard_map/while/body/eval_jaxpr/dot_general | solution.py:57
  93.1 7.4 %multiply_reduce_fusion.7 = f32[]{:T(128)} fusion(f32[48,1024]{1,0:T(8,128)S(1)} %get-tuple-element.222, f32[48,1024]{1,0:T(8,128)S(1)} %get-tuple-element.226, f32[]{:T(128)} %get-tuple-element.278, f32[1024]{0:T(1024)S(1)} %bitcast.126, f32[1024]{0:T(1024)S(1)} %bitcast.130, f32[1024]{0:T(1024)S(1)} %bitcast.122, f32[1024]{0:T(1024)S(1)} %bitcast.134, ...), kind=kOutput, calls=%fused_computation.6.clone.1.clone | convolution fusion | flops 622854144 | bytes 409616 | tf_op jit(solution)/shard_map/while/body/eval_jaxpr/dot_general | solution.py:63
  100.5 0.8 dynamic_update_slice.27
  102.5 0.7 iota_compare_fusion.6
  103.2 4.2 %multiply_reduce_fusion.6 = f32[]{:T(128)} fusion(f32[]{:T(128)} %get-tuple-element.278, f32[1024]{0:T(1024)S(1)} %bitcast.123, f32[1024]{0:T(1024)S(1)} %bitcast.127, f32[1024]{0:T(1024)S(1)} %bitcast.119, f32[1024]{0:T(1024)S(1)} %bitcast.131, f32[]{:T(128)} %get-tuple-element.275, f32[]{:T(128)} %get-tuple-element.274), kind=kLoop, calls=%fused_computation.7.clone.1.clone | loop fusion | flops 15728639 | bytes 16400 | tf_op jit(solution)/shard_map/while/body/eval_jaxpr/reduce_sum | solution.py:103
  107.4 0.8 dynamic_update_slice.26
  108.2 3.1 %bitcast_dynamic-update-slice_fusion.6 = (f32[4,48,1024]{2,1,0:T(8,128)S(1)}, f32[48,1024]{1,0:T(8,128)S(1)}) fusion(f32[4,48,1024]{2,1,0:T(8,128)S(1)} %get-tuple-element.256, s32[]{:T(128)S(6)} %copy.24, f32[]{:T(128)} %get-tuple-element.278, f32[1024]{0:T(1024)S(1)} %bitcast.124, f32[1024]{0:T(1024)S(1)} %bitcast.128, ...), kind=kOutput, calls=%fused_computation.12.clone.1.clone | convolution fusion | flops 115392512 | bytes 509452 | tf_op jit(solution)/shard_map/while/body/eval_jaxpr/dot_general | solution.py:54
  111.4 1.0 select_reduce_fusion.7
  113.1 0.7 broadcast_select_fusion.3
  113.9 4.4 %cholesky.73 = f32[48,48]{1,0:T(8,128)S(1)} custom-call(f32[48,48]{1,0:T(8,128)S(1)} %fusion.68), custom_call_target="Cholesky" | custom-call | tf_op jit(solution)/shard_map/while/body/eval_jaxpr/jit(cholesky)/cholesky | solution.py:61
  119.0 0.7 fusion.69
  119.6 3.7 %custom-call.20 = f32[1,48,48]{1,2,0:T(8,128)S(1)} custom-call(f32[1,48,48]{2,1,0:T(8,128)S(1)} %fusion.69), custom_call_target="InvertDiagBlocksLowerTriangular" | custom-call | tf_op jit(solution)/shard_map/while/body/eval_jaxpr/jit(_cho_solve)/triangular_solve | solution.py:62
  123.3 3.2 %fusion.67 = f32[48,1024]{1,0:T(8,128)S(1)} fusion(f32[]{:T(128)} %get-tuple-element.278, f32[1024]{0:T(1024)S(1)} %bitcast.125, f32[1024]{0:T(1024)S(1)} %bitcast.129, f32[1024]{0:T(1024)S(1)} %bitcast.121, f32[1024]{0:T(1024)S(1)} %bitcast.133, f32[]{:T(128)} %get-tuple-element.275, f32[]{:T(128)} %get-tuple-element.274, ...), kind=kOutput, calls=%fused_computation.9.clone.1.clone | convolution fusion | flops 115392512 | bytes 409612 | tf_op jit(solution)/shard_map/while/body/eval_jaxpr/dot_general | solution.py:57
  127.2 7.4 %multiply_reduce_fusion.7 = f32[]{:T(128)} fusion(f32[48,1024]{1,0:T(8,128)S(1)} %get-tuple-element.222, f32[48,1024]{1,0:T(8,128)S(1)} %get-tuple-element.226, f32[]{:T(128)} %get-tuple-element.278, f32[1024]{0:T(1024)S(1)} %bitcast.126, f32[1024]{0:T(1024)S(1)} %bitcast.130, f32[1024]{0:T(1024)S(1)} %bitcast.122, f32[1024]{0:T(1024)S(1)} %bitcast.134, ...), kind=kOutput, calls=%fused_computation.6.clone.1.clone | convolution fusion | flops 622854144 | bytes 409616 | tf_op jit(solution)/shard_map/while/body/eval_jaxpr/dot_general | solution.py:63
  134.5 0.8 dynamic_update_slice.27
  136.5 0.7 iota_compare_fusion.6
  137.2 4.2 %multiply_reduce_fusion.6 = f32[]{:T(128)} fusion(f32[]{:T(128)} %get-tuple-element.278, f32[1024]{0:T(1024)S(1)} %bitcast.123, f32[1024]{0:T(1024)S(1)} %bitcast.127, f32[1024]{0:T(1024)S(1)} %bitcast.119, f32[1024]{0:T(1024)S(1)} %bitcast.131, f32[]{:T(128)} %get-tuple-element.275, f32[]{:T(128)} %get-tuple-element.274), kind=kLoop, calls=%fused_computation.7.clone.1.clone | loop fusion | flops 15728639 | bytes 16400 | tf_op jit(solution)/shard_map/while/body/eval_jaxpr/reduce_sum | solution.py:103
  141.5 0.8 dynamic_update_slice.26
  142.3 3.1 %bitcast_dynamic-update-slice_fusion.6 = (f32[4,48,1024]{2,1,0:T(8,128)S(1)}, f32[48,1024]{1,0:T(8,128)S(1)}) fusion(f32[4,48,1024]{2,1,0:T(8,128)S(1)} %get-tuple-element.256, s32[]{:T(128)S(6)} %copy.24, f32[]{:T(128)} %get-tuple-element.278, f32[1024]{0:T(1024)S(1)} %bitcast.124, f32[1024]{0:T(1024)S(1)} %bitcast.128, ...), kind=kOutput, calls=%fused_computation.12.clone.1.clone | convolution fusion | flops 115392512 | bytes 509452 | tf_op jit(solution)/shard_map/while/body/eval_jaxpr/dot_general | solution.py:54
  145.4 1.0 select_reduce_fusion.7
  147.1 0.7 broadcast_select_fusion.3
  147.9 4.4 %cholesky.73 = f32[48,48]{1,0:T(8,128)S(1)} custom-call(f32[48,48]{1,0:T(8,128)S(1)} %fusion.68), custom_call_target="Cholesky" | custom-call | tf_op jit(solution)/shard_map/while/body/eval_jaxpr/jit(cholesky)/cholesky | solution.py:61
  153.0 0.7 fusion.69
  153.7 3.7 %custom-call.20 = f32[1,48,48]{1,2,0:T(8,128)S(1)} custom-call(f32[1,48,48]{2,1,0:T(8,128)S(1)} %fusion.69), custom_call_target="InvertDiagBlocksLowerTriangular" | custom-call | tf_op jit(solution)/shard_map/while/body/eval_jaxpr/jit(_cho_solve)/triangular_solve | solution.py:62
  157.3 3.2 %fusion.67 = f32[48,1024]{1,0:T(8,128)S(1)} fusion(f32[]{:T(128)} %get-tuple-element.278, f32[1024]{0:T(1024)S(1)} %bitcast.125, f32[1024]{0:T(1024)S(1)} %bitcast.129, f32[1024]{0:T(1024)S(1)} %bitcast.121, f32[1024]{0:T(1024)S(1)} %bitcast.133, f32[]{:T(128)} %get-tuple-element.275, f32[]{:T(128)} %get-tuple-element.274, ...), kind=kOutput, calls=%fused_computation.9.clone.1.clone | convolution fusion | flops 115392512 | bytes 409612 | tf_op jit(solution)/shard_map/while/body/eval_jaxpr/dot_general | solution.py:57
  161.2 7.4 %multiply_reduce_fusion.7 = f32[]{:T(128)} fusion(f32[48,1024]{1,0:T(8,128)S(1)} %get-tuple-element.222, f32[48,1024]{1,0:T(8,128)S(1)} %get-tuple-element.226, f32[]{:T(128)} %get-tuple-element.278, f32[1024]{0:T(1024)S(1)} %bitcast.126, f32[1024]{0:T(1024)S(1)} %bitcast.130, f32[1024]{0:T(1024)S(1)} %bitcast.122, f32[1024]{0:T(1024)S(1)} %bitcast.134, ...), kind=kOutput, calls=%fused_computation.6.clone.1.clone | convolution fusion | flops 622854144 | bytes 409616 | tf_op jit(solution)/shard_map/while/body/eval_jaxpr/dot_general | solution.py:63
  168.6 0.8 dynamic_update_slice.27
  171.2 4.2 %multiply_reduce_fusion.6 = f32[]{:T(128)} fusion(f32[]{:T(128)} %get-tuple-element.278, f32[1024]{0:T(1024)S(1)} %bitcast.123, f32[1024]{0:T(1024)S(1)} %bitcast.127, f32[1024]{0:T(1024)S(1)} %bitcast.119, f32[1024]{0:T(1024)S(1)} %bitcast.131, f32[]{:T(128)} %get-tuple-element.275, f32[]{:T(128)} %get-tuple-element.274), kind=kLoop, calls=%fused_computation.7.clone.1.clone | loop fusion | flops 15728639 | bytes 16400 | tf_op jit(solution)/shard_map/while/body/eval_jaxpr/reduce_sum | solution.py:103
  175.5 0.8 dynamic_update_slice.26
  176.3 3.1 %bitcast_dynamic-update-slice_fusion.6 = (f32[4,48,1024]{2,1,0:T(8,128)S(1)}, f32[48,1024]{1,0:T(8,128)S(1)}) fusion(f32[4,48,1024]{2,1,0:T(8,128)S(1)} %get-tuple-element.256, s32[]{:T(128)S(6)} %copy.24, f32[]{:T(128)} %get-tuple-element.278, f32[1024]{0:T(1024)S(1)} %bitcast.124, f32[1024]{0:T(1024)S(1)} %bitcast.128, ...), kind=kOutput, calls=%fused_computation.12.clone.1.clone | convolution fusion | flops 115392512 | bytes 509452 | tf_op jit(solution)/shard_map/while/body/eval_jaxpr/dot_general | solution.py:54
  179.4 1.0 select_reduce_fusion.7
  182.0 4.4 %cholesky.73 = f32[48,48]{1,0:T(8,128)S(1)} custom-call(f32[48,48]{1,0:T(8,128)S(1)} %fusion.68), custom_call_target="Cholesky" | custom-call | tf_op jit(solution)/shard_map/while/body/eval_jaxpr/jit(cholesky)/cholesky | solution.py:61
  187.0 0.7 fusion.69
  187.7 3.7 %custom-call.20 = f32[1,48,48]{1,2,0:T(8,128)S(1)} custom-call(f32[1,48,48]{2,1,0:T(8,128)S(1)} %fusion.69), custom_call_target="InvertDiagBlocksLowerTriangular" | custom-call | tf_op jit(solution)/shard_map/while/body/eval_jaxpr/jit(_cho_solve)/triangular_solve | solution.py:62
  191.4 3.2 %fusion.67 = f32[48,1024]{1,0:T(8,128)S(1)} fusion(f32[]{:T(128)} %get-tuple-element.278, f32[1024]{0:T(1024)S(1)} %bitcast.125, f32[1024]{0:T(1024)S(1)} %bitcast.129, f32[1024]{0:T(1024)S(1)} %bitcast.121, f32[1024]{0:T(1024)S(1)} %bitcast.133, f32[]{:T(128)} %get-tuple-element.275, f32[]{:T(128)} %get-tuple-element.274, ...), kind=kOutput, calls=%fused_computation.9.clone.1.clone | convolution fusion | flops 115392512 | bytes 409612 | tf_op jit(solution)/shard_map/while/body/eval_jaxpr/dot_general | solution.py:57
  195.2 7.4 %multiply_reduce_fusion.7 = f32[]{:T(128)} fusion(f32[48,1024]{1,0:T(8,128)S(1)} %get-tuple-element.222, f32[48,1024]{1,0:T(8,128)S(1)} %get-tuple-element.226, f32[]{:T(128)} %get-tuple-element.278, f32[1024]{0:T(1024)S(1)} %bitcast.126, f32[1024]{0:T(1024)S(1)} %bitcast.130, f32[1024]{0:T(1024)S(1)} %bitcast.122, f32[1024]{0:T(1024)S(1)} %bitcast.134, ...), kind=kOutput, calls=%fused_computation.6.clone.1.clone | convolution fusion | flops 622854144 | bytes 409616 | tf_op jit(solution)/shard_map/while/body/eval_jaxpr/dot_general | solution.py:63
  202.6 0.8 dynamic_update_slice.27
  204.0 11.7 %psum.60 = s32[]{:T(128)} all-reduce(s32[]{:T(128)} %select_reduce_fusion.2), channel_id=1, replica_groups=mesh['prow'=8,'pcol_0'=4,'pcol_1'=4,'pcol_2'=2] {'prow'}, use_global_device_ids=true, to_apply=%region_13.14 | all-reduce | flops 1 | bytes 8 | tf_op jit(solution)/shard_map/psum | solution.py:28
  215.6 11.8 %psum.56 = f32[]{:T(128)} all-reduce(f32[]{:T(128)} %fusion.22), channel_id=1, replica_groups=mesh['prow'=8,'pcol_0'=4,'pcol_1'=4,'pcol_2'=2] {'prow'}, use_global_device_ids=true, to_apply=%region_8.9 | all-reduce | flops 1 | bytes 8 | tf_op jit(solution)/shard_map/psum | solution.py:28
  227.4 6.9 %psum.61 = s32[]{:T(128)} all-reduce(s32[]{:T(128)} %psum.60), channel_id=1, replica_groups=mesh['prow'=8,'pcol_0'=4,'pcol_1'=4,'pcol_2'=2] {'pcol_0'}, use_global_device_ids=true, to_apply=%region_14.15 | all-reduce | flops 1 | bytes 8 | tf_op jit(solution)/shard_map/psum | solution.py:28
  234.3 8.1 %psum.57 = f32[]{:T(128)} all-reduce(f32[]{:T(128)} %psum.56), channel_id=1, replica_groups=mesh['prow'=8,'pcol_0'=4,'pcol_1'=4,'pcol_2'=2] {'pcol_0'}, use_global_device_ids=true, to_apply=%region_9.10 | all-reduce | flops 1 | bytes 8 | tf_op jit(solution)/shard_map/psum | solution.py:28
  242.4 6.2 %psum.62 = s32[]{:T(128)} all-reduce(s32[]{:T(128)} %psum.61), channel_id=1, replica_groups=mesh['prow'=8,'pcol_0'=4,'pcol_1'=4,'pcol_2'=2] {'pcol_1'}, use_global_device_ids=true, to_apply=%region_15.16 | all-reduce | flops 1 | bytes 8 | tf_op jit(solution)/shard_map/psum | solution.py:28
  248.6 7.7 %psum.58 = f32[]{:T(128)} all-reduce(f32[]{:T(128)} %psum.57), channel_id=1, replica_groups=mesh['prow'=8,'pcol_0'=4,'pcol_1'=4,'pcol_2'=2] {'pcol_1'}, use_global_device_ids=true, to_apply=%region_10.11 | all-reduce | flops 1 | bytes 8 | tf_op jit(solution)/shard_map/psum | solution.py:28
  256.3 16.5 %psum.63 = s32[1]{0:T(128)} all-reduce(s32[1]{0:T(128)} %bitcast.25), channel_id=1, replica_groups=mesh['prow'=8,'pcol_0'=4,'pcol_1'=4,'pcol_2'=2] {'pcol_2'}, use_global_device_ids=true, to_apply=%region_16.17 | all-reduce | flops 1 | bytes 8 | tf_op jit(solution)/shard_map/psum | solution.py:28
  272.8 3.1 %psum.59 = f32[]{:T(128)} all-reduce(f32[]{:T(128)} %psum.58), channel_id=1, replica_groups=mesh['prow'=8,'pcol_0'=4,'pcol_1'=4,'pcol_2'=2] {'pcol_2'}, use_global_device_ids=true, to_apply=%region_11.12 | all-reduce | flops 1 | bytes 8 | tf_op jit(solution)/shard_map/psum | solution.py:28
  277.1 1.4 select_bitcast_fusion
  (51 shorter events, 12.2 us)
Async XLA Ops:
  7.2 60.0 %copy-start = (s32[4,1,1,1]{0,3,2,1:T(1,128)S(1)}, s32[4,1,1,1]{0,3,2,1:T(1,128)}, u32[]{:S(2)}) copy-start(s32[4,1,1,1]{0,3,2,1:T(1,128)} %param.13) | copy-start | bytes 52
  7.2 57.4 %all-gather.2.cloned.1.call-start = ((), (), s32[]{:S(2)}) async-start(), calls=%async_computation.1 | async-start | bytes 3244032 | tf_op jit(solution)/shard_map/all_gather | solution.py:94
  9.4 17.5 %all-to-all-start = ((f32[32,1,1,2,1024]{4,3,2,1,0:T(2,128)}), f32[32,1,1,2,1024]{4,3,2,1,0:T(2,128)S(1)}, u32[]{:S(2)}, u32[]{:S(2)}) async-start(f32[32,1,1,2,1024]{4,3,2,1,0:T(2,128)} %broadcast_in_dim.93), calls=%async_computation | async-start | bytes 524288 | tf_op jit(solution)/shard_map/all_to_all | solution.py:19
Sparse Core Ops, SparseCore 0:
  10.5 53.9 all-gather.1
where the time goes:
time: 286 us; the launch traced here: 285 us
  blocking collectives  71.9 us (25%)
  other arithmetic  64.6 us (23%)
  matrix products  61.3 us (21%)
  waiting for transfers between devices  42.7 us (15%)
  between operations  16.2 us (6%)
  local copies, waits for them, and re-layouts  14.2 us (5%)
  starting transfers between devices  8.61 us (3%)
  loops' own time  5.85 us (2%)
    psum x8, blocking collectives, one_axis_at_a_time(): x = lax.psum(x, axis)  71.9 us
    all_gather x1, waiting for transfers between devices, per_device(): bank_whole = lax.all_gather(sketch_bank, PCOL, axis=0, tiled=True)  36.6 us
    dot_general x4, matrix products, compress(): lax.dot_general(sketched, coeffs, (((0,), (0,)), ((), ())), precision=lax...  29.4 us
    another operation x12, other arithmetic, compress(): factor = jnp.linalg.cholesky(gram)  20.2 us
    another operation x8, other arithmetic, compress(): coeffs = jax.scipy.linalg.cho_solve((factor, True), product)  17.3 us
    reduce_sum x4, other arithmetic, one_tile(): norm_sq = jnp.sum(tile_block * tile_block)  17 us
    dot_general x4, matrix products, compress(): jnp.dot(sketched.astype(jnp.bfloat16), tile_low, preferred_element_type=j...  12.7 us
    dot_general x4, matrix products, compress(): lax.dot_general(sketch, tile_low, (((1,), (1,)), ((), ())), preferred_ele...  12.6 us
  transfers between devices with their start and end apart: 2, of which 2 were waited for; matrix products, arithmetic and copies ran while one was open for 2% of the time, Pallas kernels for 0%

commit v1 on v0

v1 whole, which is shorter than its diff:
```python
import functools

import jax
import jax.numpy as jnp
from jax import lax
from jax.experimental import pallas as pl
from jax.experimental.pallas import tpu as pltpu
from jax.sharding import Mesh
from jax.sharding import PartitionSpec as P


PCOL = ("pcol_0", "pcol_1", "pcol_2")

TILE = 1024
RANKS = 48
SLOTS = 4
LOG2E = 1.4426950408889634
VMEM = pltpu.VMEM
SMEM = pltpu.SMEM


def spec(space):
    return pl.BlockSpec(memory_space=space)


def to_all(value, axes):
    copies = jnp.broadcast_to(value, (lax.axis_size(axes), *value.shape))
    return lax.all_to_all(copies, axes, split_axis=0, concat_axis=0)


def swap_cores(value):
    return lax.ppermute(value, "pcol_2", [(0, 1), (1, 0)])


def add_kernel(*refs):
    total = refs[0][...]
    for part in refs[1:-1]:
        total = total + part[...]
    refs[-1][...] = jnp.broadcast_to(total, refs[-1].shape)


def add_up(parts, out_shape):
    return pl.pallas_call(
        add_kernel,
        out_shape=jax.ShapeDtypeStruct(out_shape, jnp.float32),
        in_specs=[spec(VMEM)] * len(parts),
        out_specs=spec(VMEM),
        compiler_params=pltpu.CompilerParams(vmem_limit_bytes=1 << 20),
    )(*parts)


def from_others(value, axis):
    size = {"prow": 8, "pcol_0": 4, "pcol_1": 4, "pcol_2": 2}[axis]
    return [value] + [
        lax.ppermute(value, axis, [(i, (i + s) % size) for i in range(size)])
        for s in range(1, size)
    ]


def covariance_kernel(place, order, factors, ranks, rows, cols, low_hbm, norms, share, low, turned, xb, yb, sems):
    p, q = place[0], place[1]
    scale = factors[0]
    square = factors[1] * scale * scale
    power = scale * (-LOG2E)

    def tile(k, poly):
        points = rows[k * 8 + p]
        for g in range(8):
            turned[pl.ds(2 * g, 2), :] = points[:, g * 128 : (g + 1) * 128]
        columns = jnp.transpose(turned[...])
        for g in range(8):
            at = pl.ds(g * 128, 128)
            xb[at, :] = jnp.broadcast_to(columns[:, 2 * g : 2 * g + 1], (128, 128))
            yb[at, :] = jnp.broadcast_to(columns[:, 2 * g + 1 : 2 * g + 2], (128, 128))

        def strip(s, acc):
            at = pl.ds(pl.multiple_of(s * 16, 16), 16)
            xr = xb[at, :]
            yr = yb[at, :]
            for n in range(8):
                lanes = slice(n * 128, (n + 1) * 128)
                dx = xr - cols[0:1, lanes]
                dy = yr - cols[1:2, lanes]
                d2 = dx * dx + dy * dy
                r = d2 * lax.rsqrt(jnp.maximum(d2, 1e-30))
                v = poly(r, jnp.exp2(power * r))
                low[k, at, lanes] = v.astype(jnp.bfloat16)
                v2 = v * v
                acc = acc + (v2[0:8] + v2[8:16])
            return acc

        norms[k] = lax.fori_loop(0, 64, strip, jnp.zeros((8, 128), jnp.float32), unroll=2)

    polys = (
        lambda r, e: e,
        lambda r, e: (1.0 + scale * r) * e,
        lambda r, e: (1.0 + r * (scale + square * r)) * e,
    )

    def slot(k, carry):
        rank_sum, acc = carry
        i = k * 8 + p
        norms[k] = jnp.zeros((8, 128), jnp.float32)
        for which in range(3):

            @pl.when((q <= i) & (order[0] == which))
            def _(which=which):
                tile(k, polys[which])

        @pl.when(q <= i)
        def _():
            pltpu.make_async_copy(low.at[k], low_hbm.at[k], sems.at[k]).start()

        acc = acc + jnp.where(q < i, 2.0, 1.0) * norms[k]
        return rank_sum + jnp.where(q < i, ranks[k], 0), acc

    rank_sum, acc = lax.fori_loop(
        0, SLOTS, slot, (jnp.int32(0), jnp.zeros((8, 128), jnp.float32))
    )
    for k in range(SLOTS):

        @pl.when(q <= k * 8 + p)
        def _(k=k):
            pltpu.make_async_copy(low.at[k], low_hbm.at[k], sems.at[k]).wait()

    acc = jnp.sum(acc, axis=0, keepdims=True)
    lane = lax.broadcasted_iota(jnp.int32, (1, 128), 1)
    both = jnp.concatenate([acc, jnp.where(lane == 0, rank_sum.astype(jnp.float32), 0.0)], 0)
    share[...] = both[None]


def select_kernel(place, their_ids, held, theirs, sems):
    c = place[2]

    def each(act):
        for k in range(SLOTS):
            e = their_ids[k]

            @pl.when((e & 1) == c)
            def _(k=k, e=e):
                act(pltpu.make_async_copy(held.at[e // 2], theirs.at[k], sems.at[k]))

    each(lambda copy: copy.start())
    each(lambda copy: copy.wait())


def split3(value):
    high = value.astype(jnp.bfloat16)
    rest = value - high.astype(jnp.float32)
    mid = rest.astype(jnp.bfloat16)
    return high, mid, (rest - mid.astype(jnp.float32)).astype(jnp.bfloat16)


def dot_nt(a, b, **kw):
    return lax.dot_general(
        a, b, (((1,), (1,)), ((), ())), preferred_element_type=jnp.float32, **kw
    )


def three_pass(parts_a, parts_b, dot):
    n = RANKS
    one = dot(jnp.concatenate(parts_a, 0), parts_b[0])
    two = dot(jnp.concatenate(parts_a[:2], 0), parts_b[1])
    three = dot(parts_a[0], parts_b[2])
    return one[0:n] + (one[n : 2 * n] + two[0:n]) + (one[2 * n :] + two[n:] + three)


HALF = 64


def inverses(pairs, panel):
    whole = (RANKS, 2 * HALF)
    lane = lax.broadcasted_iota(jnp.int32, (1, 2 * HALF), 1)
    column = lane & (HALF - 1)
    side = lax.broadcasted_iota(jnp.int32, whole, 1) & HALF
    sub = lax.broadcasted_iota(jnp.int32, (RANKS, 1), 0)
    pairs = list(pairs)
    for start in range(0, RANKS, panel):
        cols = [
            [
                jnp.take_along_axis(m, side + (start + j), axis=1, mode="promise_in_bounds")
                for j in range(panel)
            ]
            for m in pairs
        ]
        for j in range(panel):
            k = start + j
            for t in range(len(pairs)):
                a = pairs[t]
                col = cols[t][j]
                d = 1.0 / col[k : k + 1, :]
                row = jnp.where(column == k, d, a[k : k + 1, :] * d)
                for later in range(j + 1, panel):
                    factor = cols[t][later][k : k + 1, :] * d
                    cols[t][later] = jnp.where(
                        sub == k, factor, cols[t][later] - col * factor
                    )
                pairs[t] = jnp.where(
                    sub == k, row, jnp.where(column == k, 0.0, a) - col * row
                )
    return pairs


def compress_kernel(
    place, ids, ranks, low_hbm, held, got, y_out, c_out, err_out,
    low, sk, w_all, h_all, zt, cz, sems, low_sems,
):
    p, q, c = place[0], place[1], place[2]
    dot = functools.partial(jnp.dot, preferred_element_type=jnp.float32)

    def slot_of(k):
        return k, q < k * 8 + p

    def each(act):
        for k in range(SLOTS):
            a, active = slot_of(k)
            e = ids[a]

            @pl.when(active & ((e & 1) == c))
            def _(k=k, e=e):
                act(pltpu.make_async_copy(held.at[e // 2], sk.at[k], sems.at[k]))

            @pl.when(active & ((e & 1) != c))
            def _(k=k, a=a):
                act(pltpu.make_async_copy(got.at[a], sk.at[k], sems.at[k]))

    each(lambda copy: copy.start())
    loads = [
        pltpu.make_async_copy(low_hbm.at[k], low.at[k], low_sems.at[k]) for k in range(SLOTS)
    ]
    for k in range(SLOTS):
        pl.when(slot_of(k)[1])(loads[k].start)
    r2 = lax.broadcasted_iota(jnp.int32, (RANKS, RANKS), 0)
    c2 = lax.broadcasted_iota(jnp.int32, (RANKS, RANKS), 1)
    diag = r2 == c2
    for k in range(SLOTS):
        a, active = slot_of(k)

        @pl.when(jnp.logical_not(active))
        def _():
            y_out[a] = jnp.zeros((RANKS, TILE), jnp.float32)
            c_out[a] = jnp.zeros((RANKS, TILE), jnp.float32)
            h_all[k // 2, :, pl.ds(HALF * (k % 2), RANKS)] = jnp.where(diag, 1.0, 0.0)

    each(lambda copy: copy.wait())

    for k in range(SLOTS):
        a, active = slot_of(k)

        @pl.when(active)
        def _(k=k, a=a):
            loads[k].wait()
            rank = ranks[a]
            row = lax.broadcasted_iota(jnp.int32, (RANKS, TILE), 0)
            chosen = jnp.where(row < rank, sk[k].astype(jnp.float32), 0.0).astype(jnp.bfloat16)
            sketched = jnp.transpose(dot_nt(low[k], chosen))
            y_out[a] = sketched
            parts = split3(sketched)
            w_all[k] = dot(parts[0], low[k])
            gram = three_pass(parts, parts, dot_nt)
            trace = jnp.sum(jnp.where(diag, gram, 0.0))
            mu = 0.1 * trace / rank.astype(jnp.float32)
            h_all[k // 2, :, pl.ds(HALF * (k % 2), RANKS)] = gram + jnp.where(
                diag, jnp.where(r2 < rank, mu, 1.0), 0.0
            )

    lanes = lax.broadcasted_iota(jnp.int32, (RANKS, 2 * HALF), 1)
    used = (lanes & (HALF - 1)) < RANKS
    pairs = [jnp.where(used, h_all[t], 0.0) for t in range(SLOTS // 2)]
    for t, inverse in enumerate(inverses(pairs, 4)):
        h_all[t] = inverse

    for k in range(SLOTS):
        a, active = slot_of(k)
        err_out[k] = jnp.zeros((8, 128), jnp.float32)

        @pl.when(active)
        def _(k=k, a=a):
            inverse = h_all[k // 2, :, pl.ds(HALF * (k % 2), RANKS)]
            coeffs = three_pass(split3(inverse), split3(w_all[k]), dot)
            c_out[a] = coeffs
            ch, cm, _unused = split3(coeffs)
            cz[...] = jnp.concatenate([ch, cm, ch], 0)
            yh, ym, _unused = split3(y_out[a])
            zt[...] = jnp.transpose(jnp.concatenate([yh, yh, ym], 0))
            acc = jnp.zeros((8, 128), jnp.float32)
            for n in range(4):
                lanes = slice(n * 256, (n + 1) * 256)
                approx = dot(zt[...], cz[:, lanes])
                rest = low[k, :, lanes].astype(jnp.float32) - approx
                rest = rest * rest
                rest = rest[:, :128] + rest[:, 128:]
                acc = acc + jnp.sum(rest.reshape(128, 8, 128), axis=0)
            err_out[k] = acc


def error_kernel(place, total, norms, errs, out, rank_out):
    p, q = place[0], place[1]
    summed = jnp.sum(total[...], axis=0)
    whole = jnp.sum(summed[0:1, :])
    lane = lax.broadcasted_iota(jnp.int32, (1, 128), 1)
    values = jnp.zeros((1, 128), jnp.float32)
    for k in range(SLOTS):
        i = k * 8 + p
        kept = jnp.where(q < i, jnp.sum(errs[k]), jnp.where(q == i, jnp.sum(norms[k]), 0.0))
        values = jnp.where(lane == k, kept, values)
    result = 32.0 * jnp.sqrt(values) / jnp.sqrt(jnp.full((1, 128), whole, jnp.float32))
    out[...] = result[:, :SLOTS]
    rank_out[0] = jnp.sum(summed[1:2, :]).astype(jnp.int32)


def device_program(points, range_length, smoothness, sketch_bank, sketch_ids, tile_ranks):
    f32, bf16, i32 = jnp.float32, jnp.bfloat16, jnp.int32
    shape = jax.ShapeDtypeStruct
    p = lax.axis_index("prow")
    y, x, c = (lax.axis_index(n) for n in PCOL)
    place = jnp.stack([p, (y * 4 + x) * 2 + c, c]).astype(i32)
    s = smoothness[0]
    factors = jnp.stack(
        [
            jnp.sqrt(2.0 * s.astype(f32) + 1.0) / range_length[0],
            jnp.float32(1.0 / 3.0),
        ]
    )
    ids = sketch_ids.reshape(SLOTS)
    ranks = tile_ranks.reshape(SLOTS)
    own = points.reshape(2, TILE)

    order = smoothness.astype(i32)
    rows = to_all(own, PCOL)
    held = to_all(sketch_bank[0], ("pcol_0", "pcol_1"))
    their_ids = swap_cores(ids)

    low, norms, share = pl.pallas_call(
        covariance_kernel,
        out_shape=(
            shape((SLOTS, TILE, TILE), bf16),
            shape((SLOTS, 8, 128), f32),
            shape((1, 2, 128), f32),
        ),
        in_specs=[spec(SMEM)] * 4 + [spec(VMEM)] * 2,
        out_specs=[spec(pltpu.HBM)] + [spec(VMEM)] * 2,
        scratch_shapes=[
            VMEM((SLOTS, TILE, TILE), bf16),
            VMEM((128, 128), f32),
            VMEM((TILE, 128), f32),
            VMEM((TILE, 128), f32),
            pltpu.SemaphoreType.DMA((SLOTS,)),
        ],
        compiler_params=pltpu.CompilerParams(vmem_limit_bytes=50 << 20),
        cost_estimate=pl.CostEstimate(
            flops=100_000_000, bytes_accessed=8 << 20, transcendentals=8 << 20
        ),
        name="covariance",
    )(place, order, factors, ranks, rows, own)

    small = (1, 2, 128)
    share = add_up(from_others(share, "pcol_2"), small)
    share = add_up(from_others(share, "pcol_1"), small)
    share = from_others(share, "pcol_0")
    again = add_up(share, (8, 2, 128))

    theirs = pl.pallas_call(
        select_kernel,
        out_shape=shape((SLOTS, RANKS, TILE), bf16),
        in_specs=[spec(SMEM)] * 2 + [spec(pl.ANY)],
        out_specs=spec(VMEM),
        scratch_shapes=[pltpu.SemaphoreType.DMA((SLOTS,))],
        compiler_params=pltpu.CompilerParams(vmem_limit_bytes=4 << 20),
        name="select",
    )(place, their_ids, held)
    got = swap_cores(theirs)
    total = lax.all_to_all(again, "prow", split_axis=0, concat_axis=0)

    y_all, c_all, errs = pl.pallas_call(
        compress_kernel,
        out_shape=(
            shape((SLOTS, RANKS, TILE), f32),
            shape((SLOTS, RANKS, TILE), f32),
            shape((SLOTS, 8, 128), f32),
        ),
        in_specs=[spec(SMEM)] * 3 + [spec(pltpu.HBM)] + [spec(pl.ANY)] * 2,
        out_specs=[spec(VMEM)] * 3,
        scratch_shapes=[
            VMEM((SLOTS, TILE, TILE), bf16),
            VMEM((SLOTS, RANKS, TILE), bf16),
            VMEM((SLOTS, RANKS, TILE), f32),
            VMEM((SLOTS // 2, RANKS, 2 * HALF), f32),
            VMEM((TILE, 3 * RANKS), bf16),
            VMEM((3 * RANKS, TILE), bf16),
            pltpu.SemaphoreType.DMA((SLOTS,)),
            pltpu.SemaphoreType.DMA((SLOTS,)),
        ],
        compiler_params=pltpu.CompilerParams(vmem_limit_bytes=60 << 20),
        cost_estimate=pl.CostEstimate(
            flops=2_000_000_000, bytes_accessed=8 << 20, transcendentals=0
        ),
        name="compress",
    )(place, ids, ranks, low, held, got)

    errors, rank_out = pl.pallas_call(
        error_kernel,
        out_shape=(shape((1, SLOTS), f32), shape((1,), i32)),
        in_specs=[spec(SMEM)] + [spec(VMEM)] * 3,
        out_specs=[spec(VMEM), spec(SMEM)],
        compiler_params=pltpu.CompilerParams(vmem_limit_bytes=4 << 20),
        name="errors",
    )(place, total, norms, errs)

    wide = (SLOTS, 1, 1, 1, RANKS, TILE)
    return (
        y_all.reshape(wide),
        c_all.reshape(wide),
        errors.reshape(SLOTS, 1, 1, 1),
        rank_out,
    )


def solution(mesh):
    split = Mesh(
        mesh.devices.reshape(mesh.shape["prow"], 4, 4, 2), ("prow", "pcol_0", "pcol_1", "pcol_2")
    )
    placed = (
        P(None, PCOL, None, None),
        P(),
        P(),
        P(PCOL, None, None),
        P(None, "prow", None, PCOL),
        P(None, "prow", None, PCOL),
    )
    return jax.shard_map(
        device_program,
        mesh=split,
        in_specs=placed,
        out_specs=(
            P(None, "prow", None, PCOL, None, None),
            P(None, "prow", None, PCOL, None, None),
            P(None, "prow", None, PCOL),
            P(),
        ),
        check_vma=False,
    )
```

time: 286 us -> 110 us (0.38)
  the two profiles are of different devices: /device:TPU:1 before, /device:TPU:32 now
where the time goes in v1:
time: 110 us; the launch traced here: 109 us
  waiting for transfers between devices  40.9 us (37%)
  Pallas kernels  35.7 us (32%)
  starting transfers between devices  25.5 us (23%)
  local copies, waits for them, and re-layouts  4.54 us (4%)
  between operations  2.33 us (2%)
    all_to_all x2, waiting for transfers between devices, to_all(): return lax.all_to_all(copies, axes, split_axis=0, concat_axis=0)  30.6 us
    pallas_call x1, Pallas kernels, device_program(): pl.pallas_call(compress_kernel, out_shape=(shape((SLOTS, RANKS, TILE), f3...  20.1 us
    pallas_call x1, Pallas kernels, device_program(): pl.pallas_call(covariance_kernel, out_shape=(shape((SLOTS, TILE, TILE), b...  12.8 us
    all_to_all x2, starting transfers between devices, to_all(): return lax.all_to_all(copies, axes, split_axis=0, concat_axis=0)  11 us
    all_to_all x1, starting transfers between devices, device_program(): total = lax.all_to_all(again, 'prow', split_axis=0, concat_axis=0)  9.79 us
    ppermute x7, waiting for transfers between devices, from_others(): lax.ppermute(value, axis, [(i, (i + s) % size) for i in range(size)])  9.26 us
    ppermute x7, starting transfers between devices, from_others(): lax.ppermute(value, axis, [(i, (i + s) % size) for i in range(size)])  4.5 us
    broadcast_in_dim x2, local copies, waits for them, and re-layouts, to_all(): copies = jnp.broadcast_to(value, (lax.axis_size(axes), *value.shape))  3.03 us
  transfers between devices with their start and end apart: 12, of which 10 were waited for; matrix products, arithmetic and copies ran while one was open for 1% of the time, Pallas kernels for 31%

profile of v1, /device:TPU:32, one launch (start us, length us, event | category | flops | bytes accessed | tf_op | source)
XLA Modules:
  0.0 109.1 jit_solution(10457206761198776371)
XLA Ops:
  0.6 2.3 %broadcast_in_dim.7 = bf16[16,48,1024]{2,1,0:T(8,128)(2,1)} broadcast(bf16[48,1024]{1,0:T(8,128)(2,1)} %bitcast.18), dimensions={1,2} | broadcast | bytes 1671168 | tf_op jit(solution)/shard_map/broadcast_in_dim | solution.py:27
  2.9 0.0 copy-start.7
  2.9 7.2 %all-to-all-start.1 = ((bf16[16,48,1024]{2,1,0:T(8,128)(2,1)}), bf16[16,48,1024]{2,1,0:T(8,128)(2,1)S(1)}, u32[]{:S(2)}, u32[]{:S(2)}) async-start(bf16[16,48,1024]{2,1,0:T(8,128)(2,1)} %broadcast_in_dim.7), calls=%async_computation.1 | async-start | bytes 3145728 | tf_op jit(solution)/shard_map/all_to_all | solution.py:28
  10.1 0.0 copy-start.4
  10.1 0.0 copy-start.5
  10.1 0.0 copy-done.7
  10.1 0.1 collective-permute-start
  10.2 0.1 pad_add_fusion.place
  10.3 0.0 copy-start.2
  10.3 1.1 collective-permute-done.their_ids
  11.3 23.2 %all-to-all-done.1.held = bf16[16,48,1024]{2,1,0:T(8,128)(2,1)S(1)} async-done(((bf16[16,48,1024]{2,1,0:T(8,128)(2,1)}), bf16[16,48,1024]{2,1,0:T(8,128)(2,1)S(1)}, u32[]{:S(2)}, u32[]{:S(2)}) %all-to-all-start.1) | async-done | bytes 1572896 | tf_op jit(solution)/shard_map/all_to_all | solution.py:28
  34.6 0.0 copy-start
  34.6 1.0 select.1
  35.6 0.1 collective-permute-start.1
  35.7 0.0 copy-done.4
  35.7 0.8 broadcast_in_dim.6
  36.5 3.9 %all-to-all-start = ((f32[32,2,1024]{2,1,0:T(2,128)}), f32[32,2,1024]{2,1,0:T(2,128)S(1)}, u32[]{:S(2)}, u32[]{:S(2)}) async-start(f32[32,2,1024]{2,1,0:T(2,128)} %broadcast_in_dim.6), calls=%async_computation | async-start | bytes 524288 | tf_op jit(solution)/shard_map/all_to_all | solution.py:28
  41.8 0.1 pad_maximum_fusion.factors
  41.8 7.3 %all-to-all-done.rows = f32[32,2,1024]{2,1,0:T(2,128)S(1)} async-done(((f32[32,2,1024]{2,1,0:T(2,128)}), f32[32,2,1024]{2,1,0:T(2,128)S(1)}, u32[]{:S(2)}, u32[]{:S(2)}) %all-to-all-start) | async-done | bytes 262176 | tf_op jit(solution)/shard_map/all_to_all | solution.py:28
  49.2 0.0 copy-done.5
  49.2 12.8 %covariance.1 = (bf16[4,1024,1024]{2,1,0:T(8,128)(2,1)}, f32[4,8,128]{2,1,0:T(8,128)S(1)}, f32[1,2,128]{2,1,0:T(2,128)S(1)}) custom-call(s32[3]{0:T(128)S(1)} %pad_add_fusion.place, s32[1]{0:T(128)S(6)} %copy.13.order, f32[2]{0:T(128)S(1)} %pad_maximum_fusion.factors, s32[4]{0:T(128)S(1)} %bitcast.17, f32[32,2,1024]{2,1,0:T(2,128)S(1)} %all-to-all-done.rows, ...), custom_call_target="tpu_custom_call" | custom-call | flops 100000000 | bytes 8388608 | tf_op jit(solution)/shard_map/covariance/pallas_call | solution.py:334
  62.0 0.0 copy-done.2
  62.0 0.0 copy-done
  62.0 0.5 collective-permute-start.2
  62.5 0.8 collective-permute-done.2.refs_1_
  63.3 0.0 collective-permute-start.5
  63.3 0.1 collective-permute-start.4
  63.4 1.9 %collective-permute-start.3 = (f32[1,2,128]{2,1,0:T(2,128)S(1)}, f32[1,2,128]{2,1,0:T(2,128)S(1)}, u32[]{:S(2)}, u32[]{:S(2)}) collective-permute-start(f32[1,2,128]{2,1,0:T(2,128)S(1)} %shard_map.93.refs_0_), channel_id=1, source_target_pairs={{0,2},{2,4},{4,6},{6,0},{1,3},{3,5},{5,7},{7,1},{8,10},{10,12},{12... | collective-permute-start | bytes 3080 | tf_op jit(solution)/shard_map/ppermute | solution.py:55
  65.3 1.5 %collective-permute-done.5.refs_3_ = f32[1,2,128]{2,1,0:T(2,128)S(1)} collective-permute-done((f32[1,2,128]{2,1,0:T(2,128)S(1)}, f32[1,2,128]{2,1,0:T(2,128)S(1)}, u32[]{:S(2)}, u32[]{:S(2)}) %collective-permute-start.5) | collective-permute-done | bytes 1056 | tf_op jit(solution)/shard_map/ppermute | solution.py:55
  66.8 1.5 %collective-permute-done.4.refs_2_ = f32[1,2,128]{2,1,0:T(2,128)S(1)} collective-permute-done((f32[1,2,128]{2,1,0:T(2,128)S(1)}, f32[1,2,128]{2,1,0:T(2,128)S(1)}, u32[]{:S(2)}, u32[]{:S(2)}) %collective-permute-start.4) | collective-permute-done | bytes 1056 | tf_op jit(solution)/shard_map/ppermute | solution.py:55
  68.4 1.2 %collective-permute-done.3.refs_1_ = f32[1,2,128]{2,1,0:T(2,128)S(1)} collective-permute-done((f32[1,2,128]{2,1,0:T(2,128)S(1)}, f32[1,2,128]{2,1,0:T(2,128)S(1)}, u32[]{:S(2)}, u32[]{:S(2)}) %collective-permute-start.3) | collective-permute-done | bytes 1056 | tf_op jit(solution)/shard_map/ppermute | solution.py:55
  69.5 0.0 collective-permute-start.8
  69.5 0.1 collective-permute-start.7
  69.6 1.9 %collective-permute-start.6 = (f32[1,2,128]{2,1,0:T(2,128)S(1)}, f32[1,2,128]{2,1,0:T(2,128)S(1)}, u32[]{:S(2)}, u32[]{:S(2)}) collective-permute-start(f32[1,2,128]{2,1,0:T(2,128)S(1)} %shard_map.94.refs_0_), channel_id=1, source_target_pairs={{0,8},{8,16},{16,24},{24,0},{1,9},{9,17},{17,25},{25,1},{2,10},{10... | collective-permute-start | bytes 3080 | tf_op jit(solution)/shard_map/ppermute | solution.py:55
  71.6 1.5 %collective-permute-done.8.refs_3_ = f32[1,2,128]{2,1,0:T(2,128)S(1)} collective-permute-done((f32[1,2,128]{2,1,0:T(2,128)S(1)}, f32[1,2,128]{2,1,0:T(2,128)S(1)}, u32[]{:S(2)}, u32[]{:S(2)}) %collective-permute-start.8) | collective-permute-done | bytes 1056 | tf_op jit(solution)/shard_map/ppermute | solution.py:55
  73.1 1.6 %collective-permute-done.7.refs_2_ = f32[1,2,128]{2,1,0:T(2,128)S(1)} collective-permute-done((f32[1,2,128]{2,1,0:T(2,128)S(1)}, f32[1,2,128]{2,1,0:T(2,128)S(1)}, u32[]{:S(2)}, u32[]{:S(2)}) %collective-permute-start.7) | collective-permute-done | bytes 1056 | tf_op jit(solution)/shard_map/ppermute | solution.py:55
  74.7 1.1 collective-permute-done.6.refs_1_
  75.8 0.6 shard_map.95
  76.4 9.8 %all-to-all-start.2 = ((f32[8,2,128]{2,1,0:T(2,128)}), f32[8,2,128]{2,1,0:T(2,128)S(1)}, u32[]{:S(2)}, u32[]{:S(2)}) async-start(f32[8,2,128]{2,1,0:T(2,128)} %shard_map.95), calls=%async_computation.2 | async-start | bytes 16384 | tf_op jit(solution)/shard_map/all_to_all | solution.py:373
  86.2 0.0 collective-permute-done.1.got
  86.2 0.0 copy-start.6
  86.2 0.8 copy-done.6
  87.0 0.0 copy-start.3
  87.0 20.1 %compress.1 = (f32[4,48,1024]{2,1,0:T(8,128)}, f32[4,48,1024]{2,1,0:T(8,128)}, f32[4,8,128]{2,1,0:T(8,128)}) custom-call(s32[3]{0:T(128)} %copy-done.2, s32[4]{0:T(128)} %bitcast.19, s32[4]{0:T(128)} %bitcast.16, bf16[4,1024,1024]{2,1,0:T(8,128)(2,1)} %get-tuple-element.12.low_hbm, bf16[16,48,1024]{2,1,0:T(8,128)(2,1)} %copy-done, bf16[4,48,1024]{2,1,0:T(8,128)(2,1)} %copy-done.6), custom_call_target="tpu_custom_call" | custom-call | flops 2000000000 | bytes 8388608 | tf_op jit(solution)/shard_map/compress/pallas_call | solution.py:375
  107.0 0.0 all-to-all-done.2.total
  107.0 0.0 copy-done.3
  107.1 0.0 copy-start.1
  107.1 0.7 copy-done.1
  107.8 1.2 %errors.1 = (f32[1,4]{1,0:T(1,128)}, s32[1]{0:T(128)}) custom-call(s32[3]{0:T(128)S(1)} %copy-done.3, f32[8,2,128]{2,1,0:T(2,128)S(1)} %all-to-all-done.2.total, f32[4,8,128]{2,1,0:T(8,128)S(1)} %get-tuple-element.16.norms, f32[4,8,128]{2,1,0:T(8,128)S(1)} %copy-done.1), custom_call_target="tpu_custom_call" | custom-call | tf_op jit(solution)/shard_map/errors/pallas_call | solution.py:401
  (2 shorter events, 0.0 us)
Async XLA Ops:
  2.9 7.2 %copy-start.7 = (s32[4,1,1,1]{0,3,2,1:T(1,128)S(1)}, s32[4,1,1,1]{0,3,2,1:T(1,128)}, u32[]{:S(2)}) copy-start(s32[4,1,1,1]{0,3,2,1:T(1,128)} %param.10) | copy-start | bytes 52
  2.9 31.7 %all-to-all-start.1 = ((bf16[16,48,1024]{2,1,0:T(8,128)(2,1)}), bf16[16,48,1024]{2,1,0:T(8,128)(2,1)S(1)}, u32[]{:S(2)}, u32[]{:S(2)}) async-start(bf16[16,48,1024]{2,1,0:T(8,128)(2,1)} %broadcast_in_dim.7), calls=%async_computation.1 | async-start | bytes 3145728 | tf_op jit(solution)/shard_map/all_to_all | solution.py:28
  10.1 25.7 %copy-start.4 = (f32[1,1,2,1024]{3,2,1,0:T(2,128)S(1)}, f32[1,1,2,1024]{3,2,1,0:T(2,128)}, u32[]{:S(2)}) copy-start(f32[1,1,2,1024]{3,2,1,0:T(2,128)} %param.6) | copy-start | bytes 24580
  10.1 39.1 %copy-start.5 = (s32[4,1,1,1]{0,3,2,1:T(1,128)S(1)}, s32[4,1,1,1]{0,3,2,1:T(1,128)}, u32[]{:S(2)}) copy-start(s32[4,1,1,1]{0,3,2,1:T(1,128)} %param.11) | copy-start | bytes 52
  10.1 1.2 %collective-permute-start = (s32[4]{0:T(128)S(1)}, s32[4]{0:T(128)S(1)}, u32[]{:S(2)}, u32[]{:S(2)}) collective-permute-start(s32[4]{0:T(128)S(1)} %bitcast.20), channel_id=1, source_target_pairs={{0,1},{1,0},{2,3},{3,2},{4,5},{5,4},{6,7},{7,6},{8,9},{9,8},{10,11... | collective-permute-start | bytes 56 | tf_op jit(solution)/shard_map/ppermute | solution.py:32
  10.3 51.7 %copy-start.2 = (s32[3]{0:T(128)}, s32[3]{0:T(128)S(1)}, u32[]{:S(2)}) copy-start(s32[3]{0:T(128)S(1)} %pad_add_fusion.place) | copy-start | bytes 40
  34.6 27.4 %copy-start = (bf16[16,48,1024]{2,1,0:T(8,128)(2,1)}, bf16[16,48,1024]{2,1,0:T(8,128)(2,1)S(1)}, u32[]{:S(2)}) copy-start(bf16[16,48,1024]{2,1,0:T(8,128)(2,1)S(1)} %all-to-all-done.1.held) | copy-start | bytes 4718596
  35.6 50.6 %collective-permute-start.1 = (bf16[4,48,1024]{2,1,0:T(8,128)(2,1)S(1)}, bf16[4,48,1024]{2,1,0:T(8,128)(2,1)S(1)}, u32[]{:S(2)}, u32[]{:S(2)}) collective-permute-start(bf16[4,48,1024]{2,1,0:T(8,128)(2,1)S(1)} %select.1), channel_id=1, source_target_pairs={{0,1},{1,0},{2,3},{3,2},{4,5},{5,4},{6,7},{7,6},{8,9},{9,8},{10,11... | collective-permute-start | bytes 1179656 | tf_op jit(solution)/shard_map/ppermute | solution.py:32
  36.5 12.7 %all-to-all-start = ((f32[32,2,1024]{2,1,0:T(2,128)}), f32[32,2,1024]{2,1,0:T(2,128)S(1)}, u32[]{:S(2)}, u32[]{:S(2)}) async-start(f32[32,2,1024]{2,1,0:T(2,128)} %broadcast_in_dim.6), calls=%async_computation | async-start | bytes 524288 | tf_op jit(solution)/shard_map/all_to_all | solution.py:28
  62.0 1.3 %collective-permute-start.2 = (f32[1,2,128]{2,1,0:T(2,128)S(1)}, f32[1,2,128]{2,1,0:T(2,128)S(1)}, u32[]{:S(2)}, u32[]{:S(2)}) collective-permute-start(f32[1,2,128]{2,1,0:T(2,128)S(1)} %get-tuple-element.15.refs_0_), channel_id=1, source_target_pairs={{0,1},{1,0},{2,3},{3,2},{4,5},{5,4},{6,7},{7,6},{8,9},{9,8},{10,11... | collective-permute-start | bytes 3080 | tf_op jit(solution)/shard_map/ppermute | solution.py:55
  63.3 3.6 %collective-permute-start.5 = (f32[1,2,128]{2,1,0:T(2,128)S(1)}, f32[1,2,128]{2,1,0:T(2,128)S(1)}, u32[]{:S(2)}, u32[]{:S(2)}) collective-permute-start(f32[1,2,128]{2,1,0:T(2,128)S(1)} %shard_map.93.refs_0_), channel_id=1, source_target_pairs={{0,6},{2,0},{4,2},{6,4},{1,7},{3,1},{5,3},{7,5},{8,14},{10,8},{12,... | collective-permute-start | bytes 3080 | tf_op jit(solution)/shard_map/ppermute | solution.py:55
  63.3 5.1 %collective-permute-start.4 = (f32[1,2,128]{2,1,0:T(2,128)S(1)}, f32[1,2,128]{2,1,0:T(2,128)S(1)}, u32[]{:S(2)}, u32[]{:S(2)}) collective-permute-start(f32[1,2,128]{2,1,0:T(2,128)S(1)} %shard_map.93.refs_0_), channel_id=1, source_target_pairs={{0,4},{2,6},{4,0},{6,2},{1,5},{3,7},{5,1},{7,3},{8,12},{10,14},{12... | collective-permute-start | bytes 3080 | tf_op jit(solution)/shard_map/ppermute | solution.py:55
  63.4 6.1 %collective-permute-start.3 = (f32[1,2,128]{2,1,0:T(2,128)S(1)}, f32[1,2,128]{2,1,0:T(2,128)S(1)}, u32[]{:S(2)}, u32[]{:S(2)}) collective-permute-start(f32[1,2,128]{2,1,0:T(2,128)S(1)} %shard_map.93.refs_0_), channel_id=1, source_target_pairs={{0,2},{2,4},{4,6},{6,0},{1,3},{3,5},{5,7},{7,1},{8,10},{10,12},{12... | collective-permute-start | bytes 3080 | tf_op jit(solution)/shard_map/ppermute | solution.py:55
  69.5 3.6 %collective-permute-start.8 = (f32[1,2,128]{2,1,0:T(2,128)S(1)}, f32[1,2,128]{2,1,0:T(2,128)S(1)}, u32[]{:S(2)}, u32[]{:S(2)}) collective-permute-start(f32[1,2,128]{2,1,0:T(2,128)S(1)} %shard_map.94.refs_0_), channel_id=1, source_target_pairs={{0,24},{8,0},{16,8},{24,16},{1,25},{9,1},{17,9},{25,17},{2,26},{10... | collective-permute-start | bytes 3080 | tf_op jit(solution)/shard_map/ppermute | solution.py:55
  69.5 5.2 %collective-permute-start.7 = (f32[1,2,128]{2,1,0:T(2,128)S(1)}, f32[1,2,128]{2,1,0:T(2,128)S(1)}, u32[]{:S(2)}, u32[]{:S(2)}) collective-permute-start(f32[1,2,128]{2,1,0:T(2,128)S(1)} %shard_map.94.refs_0_), channel_id=1, source_target_pairs={{0,16},{8,24},{16,0},{24,8},{1,17},{9,25},{17,1},{25,9},{2,18},{10... | collective-permute-start | bytes 3080 | tf_op jit(solution)/shard_map/ppermute | solution.py:55
  69.6 6.1 %collective-permute-start.6 = (f32[1,2,128]{2,1,0:T(2,128)S(1)}, f32[1,2,128]{2,1,0:T(2,128)S(1)}, u32[]{:S(2)}, u32[]{:S(2)}) collective-permute-start(f32[1,2,128]{2,1,0:T(2,128)S(1)} %shard_map.94.refs_0_), channel_id=1, source_target_pairs={{0,8},{8,16},{16,24},{24,0},{1,9},{9,17},{17,25},{25,1},{2,10},{10... | collective-permute-start | bytes 3080 | tf_op jit(solution)/shard_map/ppermute | solution.py:55
  76.4 30.6 %all-to-all-start.2 = ((f32[8,2,128]{2,1,0:T(2,128)}), f32[8,2,128]{2,1,0:T(2,128)S(1)}, u32[]{:S(2)}, u32[]{:S(2)}) async-start(f32[8,2,128]{2,1,0:T(2,128)} %shard_map.95), calls=%async_computation.2 | async-start | bytes 16384 | tf_op jit(solution)/shard_map/all_to_all | solution.py:373
  86.2 0.8 copy-start.6
  87.0 20.1 %copy-start.3 = (s32[3]{0:T(128)S(1)}, s32[3]{0:T(128)}, u32[]{:S(2)}) copy-start(s32[3]{0:T(128)} %copy-done.2) | copy-start | bytes 40
  107.1 0.7 copy-start.1

commit v2 on v1

--- a/solution.py
+++ b/solution.py
@@ -10,10 +10,12 @@
 
 
 PCOL = ("pcol_0", "pcol_1", "pcol_2")
+ALL = ("prow", "pcol_0", "pcol_1", "pcol_2")
 
 TILE = 1024
 RANKS = 48
 SLOTS = 4
+PARTS = 4
 LOG2E = 1.4426950408889634
 VMEM = pltpu.VMEM
 SMEM = pltpu.SMEM
@@ -28,33 +30,57 @@
     return lax.all_to_all(copies, axes, split_axis=0, concat_axis=0)
 
 
+def plane_shift(value, shift, stage):
+    pairs = []
+    for y in range(4):
+        for x in range(4):
+            for c in range(2):
+                if (c == 0) == (stage == 0):
+                    to = (y, (x + shift) % 4, c)
+                else:
+                    to = ((y + shift) % 4, x, c)
+                pairs.append(((y * 4 + x) * 2 + c, (to[0] * 4 + to[1]) * 2 + to[2]))
+    return lax.ppermute(value, PCOL, pairs)
+
+
+def group_kernel(*refs):
+    parts, out, sems = refs[:-2], refs[-2], refs[-1]
+    moves = [pltpu.make_async_copy(part, out.at[i], sems.at[i]) for i, part in enumerate(parts)]
+    for move in moves:
+        move.start()
+    for move in moves:
+        move.wait()
+
+
+def bank_of_plane(own):
+    parts = [own] + [plane_shift(own, shift, 0) for shift in (1, 2, 3)]
+    group = pl.pallas_call(
+        group_kernel,
+        out_shape=jax.ShapeDtypeStruct((4, *own.shape), own.dtype),
+        in_specs=[spec(VMEM)] * 4,
+        out_specs=spec(pltpu.HBM),
+        scratch_shapes=[pltpu.SemaphoreType.DMA((4,))],
+        compiler_params=pltpu.CompilerParams(vmem_limit_bytes=4 << 20),
+        name="group_bank",
+    )(*parts)
+    return [group] + [plane_shift(group, shift, 1) for shift in (1, 2, 3)]
+
+
+def fetch_entry(place, entry, wanted, held, out, sem, act):
+    c, y, x = place[2], place[3], place[4]
+    dy = (y - (entry >> 3)) & 3
+    dx = (x - ((entry >> 1) & 3)) & 3
+    inner = jnp.where(c == 0, dx, dy)
+    outer = jnp.where(c == 0, dy, dx)
+    for o in range(4):
+
+        @pl.when(wanted & ((entry & 1) == c) & (outer == o))
+        def _(o=o):
+            act(pltpu.make_async_copy(held[o].at[inner], out, sem))
+
+
 def swap_cores(value):
     return lax.ppermute(value, "pcol_2", [(0, 1), (1, 0)])
-
-
-def add_kernel(*refs):
-    total = refs[0][...]
-    for part in refs[1:-1]:
-        total = total + part[...]
-    refs[-1][...] = jnp.broadcast_to(total, refs[-1].shape)
-
-
-def add_up(parts, out_shape):
-    return pl.pallas_call(
-        add_kernel,
-        out_shape=jax.ShapeDtypeStruct(out_shape, jnp.float32),
-        in_specs=[spec(VMEM)] * len(parts),
-        out_specs=spec(VMEM),
-        compiler_params=pltpu.CompilerParams(vmem_limit_bytes=1 << 20),
-    )(*parts)
-
-
-def from_others(value, axis):
-    size = {"prow": 8, "pcol_0": 4, "pcol_1": 4, "pcol_2": 2}[axis]
-    return [value] + [
-        lax.ppermute(value, axis, [(i, (i + s) % size) for i in range(size)])
-        for s in range(1, size)
-    ]
 
 
 def covariance_kernel(place, order, factors, ranks, rows, cols, low_hbm, norms, share, low, turned, xb, yb, sems):
@@ -129,18 +155,15 @@
     share[...] = both[None]
 
 
-def select_kernel(place, their_ids, held, theirs, sems):
-    c = place[2]
-
+def select_kernel(place, their_ids, share, h0, h1, h2, h3, theirs, again, sems):
     def each(act):
         for k in range(SLOTS):
-            e = their_ids[k]
-
-            @pl.when((e & 1) == c)
-            def _(k=k, e=e):
-                act(pltpu.make_async_copy(held.at[e // 2], theirs.at[k], sems.at[k]))
+            fetch_entry(
+                place, their_ids[k], True, (h0, h1, h2, h3), theirs.at[k], sems.at[k], act
+            )
 
     each(lambda copy: copy.start())
+    again[...] = jnp.broadcast_to(share[...], again.shape)
     each(lambda copy: copy.wait())
 
 
@@ -202,7 +225,7 @@
 
 
 def compress_kernel(
-    place, ids, ranks, low_hbm, held, got, y_out, c_out, err_out,
+    place, ids, ranks, low_hbm, got, h0, h1, h2, h3, y_out, c_out, err_out,
     low, sk, w_all, h_all, zt, cz, sems, low_sems,
 ):
     p, q, c = place[0], place[1], place[2]
@@ -216,20 +239,20 @@
             a, active = slot_of(k)
             e = ids[a]
 
-            @pl.when(active & ((e & 1) == c))
-            def _(k=k, e=e):
-                act(pltpu.make_async_copy(held.at[e // 2], sk.at[k], sems.at[k]))
+            fetch_entry(place, e, active, (h0, h1, h2, h3), sk.at[k], sems.at[k], act)
 
             @pl.when(active & ((e & 1) != c))
             def _(k=k, a=a):
                 act(pltpu.make_async_copy(got.at[a], sk.at[k], sems.at[k]))
 
     each(lambda copy: copy.start())
-    loads = [
-        pltpu.make_async_copy(low_hbm.at[k], low.at[k], low_sems.at[k]) for k in range(SLOTS)
-    ]
-    for k in range(SLOTS):
-        pl.when(slot_of(k)[1])(loads[k].start)
+
+    def load(k, act):
+        for m in range(PARTS):
+            part = pl.ds(m * (TILE // PARTS), TILE // PARTS)
+            act(pltpu.make_async_copy(low_hbm.at[k, part], low.at[k, part], low_sems.at[k, m]))
+
+    pl.when(slot_of(0)[1])(lambda: load(0, lambda copy: copy.start()))
     r2 = lax.broadcasted_iota(jnp.int32, (RANKS, RANKS), 0)
     c2 = lax.broadcasted_iota(jnp.int32, (RANKS, RANKS), 1)
     diag = r2 == c2
@@ -247,13 +270,17 @@
     for k in range(SLOTS):
         a, active = slot_of(k)
 
+        pl.when(active)(functools.partial(load, k, lambda copy: copy.wait()))
+        if k + 1 < SLOTS:
+            ahead = functools.partial(load, k + 1, lambda copy: copy.start())
+            pl.when(slot_of(k + 1)[1])(ahead)
+
         @pl.when(active)
         def _(k=k, a=a):
-            loads[k].wait()
             rank = ranks[a]
             row = lax.broadcasted_iota(jnp.int32, (RANKS, TILE), 0)
             chosen = jnp.where(row < rank, sk[k].astype(jnp.float32), 0.0).astype(jnp.bfloat16)
-            sketched = jnp.transpose(dot_nt(low[k], chosen))
+            sketched = dot_nt(chosen, low[k])
             y_out[a] = sketched
             parts = split3(sketched)
             w_all[k] = dot(parts[0], low[k])
@@ -267,7 +294,7 @@
     lanes = lax.broadcasted_iota(jnp.int32, (RANKS, 2 * HALF), 1)
     used = (lanes & (HALF - 1)) < RANKS
     pairs = [jnp.where(used, h_all[t], 0.0) for t in range(SLOTS // 2)]
-    for t, inverse in enumerate(inverses(pairs, 4)):
+    for t, inverse in enumerate(inverses(pairs, 8)):
         h_all[t] = inverse
 
     for k in range(SLOTS):
@@ -309,29 +336,10 @@
     rank_out[0] = jnp.sum(summed[1:2, :]).astype(jnp.int32)
 
 
-def device_program(points, range_length, smoothness, sketch_bank, sketch_ids, tile_ranks):
-    f32, bf16, i32 = jnp.float32, jnp.bfloat16, jnp.int32
+def covariance(*args):
+    f32, bf16 = jnp.float32, jnp.bfloat16
     shape = jax.ShapeDtypeStruct
-    p = lax.axis_index("prow")
-    y, x, c = (lax.axis_index(n) for n in PCOL)
-    place = jnp.stack([p, (y * 4 + x) * 2 + c, c]).astype(i32)
-    s = smoothness[0]
-    factors = jnp.stack(
-        [
-            jnp.sqrt(2.0 * s.astype(f32) + 1.0) / range_length[0],
-            jnp.float32(1.0 / 3.0),
-        ]
-    )
-    ids = sketch_ids.reshape(SLOTS)
-    ranks = tile_ranks.reshape(SLOTS)
-    own = points.reshape(2, TILE)
-
-    order = smoothness.astype(i32)
-    rows = to_all(own, PCOL)
-    held = to_all(sketch_bank[0], ("pcol_0", "pcol_1"))
-    their_ids = swap_cores(ids)
-
-    low, norms, share = pl.pallas_call(
+    return pl.pallas_call(
         covariance_kernel,
         out_shape=(
             shape((SLOTS, TILE, TILE), bf16),
@@ -352,34 +360,20 @@
             flops=100_000_000, bytes_accessed=8 << 20, transcendentals=8 << 20
         ),
         name="covariance",
-    )(place, order, factors, ranks, rows, own)
-
-    small = (1, 2, 128)
-    share = add_up(from_others(share, "pcol_2"), small)
-    share = add_up(from_others(share, "pcol_1"), small)
-    share = from_others(share, "pcol_0")
-    again = add_up(share, (8, 2, 128))
-
-    theirs = pl.pallas_call(
-        select_kernel,
-        out_shape=shape((SLOTS, RANKS, TILE), bf16),
-        in_specs=[spec(SMEM)] * 2 + [spec(pl.ANY)],
-        out_specs=spec(VMEM),
-        scratch_shapes=[pltpu.SemaphoreType.DMA((SLOTS,))],
-        compiler_params=pltpu.CompilerParams(vmem_limit_bytes=4 << 20),
-        name="select",
-    )(place, their_ids, held)
-    got = swap_cores(theirs)
-    total = lax.all_to_all(again, "prow", split_axis=0, concat_axis=0)
-
-    y_all, c_all, errs = pl.pallas_call(
+    )(*args)
+
+
+def compress(*args):
+    f32, bf16 = jnp.float32, jnp.bfloat16
+    shape = jax.ShapeDtypeStruct
+    return pl.pallas_call(
         compress_kernel,
         out_shape=(
             shape((SLOTS, RANKS, TILE), f32),
             shape((SLOTS, RANKS, TILE), f32),
             shape((SLOTS, 8, 128), f32),
         ),
-        in_specs=[spec(SMEM)] * 3 + [spec(pltpu.HBM)] + [spec(pl.ANY)] * 2,
+        in_specs=[spec(SMEM)] * 3 + [spec(pltpu.HBM)] + [spec(pl.ANY)] * 5,
         out_specs=[spec(VMEM)] * 3,
         scratch_shapes=[
             VMEM((SLOTS, TILE, TILE), bf16),
@@ -389,14 +383,53 @@
             VMEM((TILE, 3 * RANKS), bf16),
             VMEM((3 * RANKS, TILE), bf16),
             pltpu.SemaphoreType.DMA((SLOTS,)),
-            pltpu.SemaphoreType.DMA((SLOTS,)),
+            pltpu.SemaphoreType.DMA((SLOTS, PARTS)),
         ],
         compiler_params=pltpu.CompilerParams(vmem_limit_bytes=60 << 20),
         cost_estimate=pl.CostEstimate(
             flops=2_000_000_000, bytes_accessed=8 << 20, transcendentals=0
         ),
         name="compress",
-    )(place, ids, ranks, low, held, got)
+    )(*args)
+
+
+def device_program(points, range_length, smoothness, sketch_bank, sketch_ids, tile_ranks):
+    f32, bf16, i32 = jnp.float32, jnp.bfloat16, jnp.int32
+    shape = jax.ShapeDtypeStruct
+    p = lax.axis_index("prow")
+    y, x, c = (lax.axis_index(n) for n in PCOL)
+    place = jnp.stack([p, (y * 4 + x) * 2 + c, c, y, x]).astype(i32)
+    s = smoothness[0]
+    factors = jnp.stack(
+        [
+            jnp.sqrt(2.0 * s.astype(f32) + 1.0) / range_length[0],
+            jnp.float32(1.0 / 3.0),
+        ]
+    )
+    ids = sketch_ids.reshape(SLOTS)
+    ranks = tile_ranks.reshape(SLOTS)
+    own = points.reshape(2, TILE)
+
+    order = smoothness.astype(i32)
+    rows = to_all(own, PCOL)
+    held = bank_of_plane(sketch_bank[0])
+    their_ids = swap_cores(ids)
+
+    low, norms, share = covariance(place, order, factors, ranks, rows, own)
+
+    theirs, again = pl.pallas_call(
+        select_kernel,
+        out_shape=(shape((SLOTS, RANKS, TILE), bf16), shape((256, 2, 128), f32)),
+        in_specs=[spec(SMEM)] * 2 + [spec(VMEM)] + [spec(pl.ANY)] * 4,
+        out_specs=[spec(VMEM)] * 2,
+        scratch_shapes=[pltpu.SemaphoreType.DMA((SLOTS,))],
+        compiler_params=pltpu.CompilerParams(vmem_limit_bytes=4 << 20),
+        name="select",
+    )(place, their_ids, share, *held)
+    got = swap_cores(theirs)
+    total = lax.all_to_all(again, ALL, split_axis=0, concat_axis=0)
+
+    y_all, c_all, errs = compress(place, ids, ranks, low, got, *held)
 
     errors, rank_out = pl.pallas_call(
         error_kernel,

time: 110 us -> 77.4 us (0.70)
  the two profiles are of different devices: /device:TPU:32 before, /device:TPU:1 now
where the time goes in v2:
time: 77.4 us; the launch traced here: 76.9 us
  starting transfers between devices  28.4 us (37%)
  Pallas kernels  27.7 us (36%)
  waiting for transfers between devices  13 us (17%)
  local copies, waits for them, and re-layouts  5.28 us (7%)
  between operations  2.36 us (3%)
    pallas_call x1, Pallas kernels, compress(): pl.pallas_call(compress_kernel, out_shape=(shape((SLOTS, RANKS, TILE), f3...  14 us
    pallas_call x1, Pallas kernels, covariance(): pl.pallas_call(covariance_kernel, out_shape=(shape((SLOTS, TILE, TILE), b...  10.1 us
    all_to_all x1, starting transfers between devices, device_program(): total = lax.all_to_all(again, ALL, split_axis=0, concat_axis=0)  9.91 us
    ppermute x6, starting transfers between devices, plane_shift(): return lax.ppermute(value, PCOL, pairs)  8.06 us
    all_to_all x1, waiting for transfers between devices, to_all(): return lax.all_to_all(copies, axes, split_axis=0, concat_axis=0)  7 us
    all_to_all x1, starting transfers between devices, to_all(): return lax.all_to_all(copies, axes, split_axis=0, concat_axis=0)  6.96 us
    ppermute x6, waiting for transfers between devices, plane_shift(): return lax.ppermute(value, PCOL, pairs)  5.5 us
    unnamed x22, local copies, waits for them, and re-layouts  3.73 us
  transfers between devices with their start and end apart: 10, of which 5 were waited for; matrix products, arithmetic and copies ran while one was open for 2% of the time, Pallas kernels for 31%

profile of v2, /device:TPU:1, one launch (start us, length us, event | category | flops | bytes accessed | tf_op | source)
XLA Modules:
  0.0 76.9 jit_solution(18247787689289028519)
XLA Ops:
  0.6 3.6 %collective-permute-start.3 = (bf16[48,1024]{1,0:T(8,128)(2,1)}, bf16[48,1024]{1,0:T(8,128)(2,1)S(1)}, u32[]{:S(2)}, u32[]{:S(2)}) collective-permute-start(bf16[48,1024]{1,0:T(8,128)(2,1)} %bitcast.16), channel_id=1, source_target_pairs={{0,6},{1,25},{2,0},{3,27},{4,2},{5,29},{6,4},{7,31},{8,14},{9,1},{... | collective-permute-start | bytes 294920 | tf_op jit(solution)/shard_map/ppermute | solution.py:43
  4.3 0.3 collective-permute-start.2
  4.6 0.7 collective-permute-start.1
  5.3 1.9 %collective-permute-done.3.refs_3_ = bf16[48,1024]{1,0:T(8,128)(2,1)S(1)} collective-permute-done((bf16[48,1024]{1,0:T(8,128)(2,1)}, bf16[48,1024]{1,0:T(8,128)(2,1)S(1)}, u32[]{:S(2)}, u32[]{:S(2)}) %collective-permute-start.3) | collective-permute-done | bytes 98336 | tf_op jit(solution)/shard_map/ppermute | solution.py:43
  7.2 2.3 %collective-permute-done.2.refs_2_ = bf16[48,1024]{1,0:T(8,128)(2,1)S(1)} collective-permute-done((bf16[48,1024]{1,0:T(8,128)(2,1)}, bf16[48,1024]{1,0:T(8,128)(2,1)S(1)}, u32[]{:S(2)}, u32[]{:S(2)}) %collective-permute-start.2) | collective-permute-done | bytes 98336 | tf_op jit(solution)/shard_map/ppermute | solution.py:43
  9.5 1.2 %collective-permute-done.1.refs_1_ = bf16[48,1024]{1,0:T(8,128)(2,1)S(1)} collective-permute-done((bf16[48,1024]{1,0:T(8,128)(2,1)}, bf16[48,1024]{1,0:T(8,128)(2,1)S(1)}, u32[]{:S(2)}, u32[]{:S(2)}) %collective-permute-start.1) | collective-permute-done | bytes 98336 | tf_op jit(solution)/shard_map/ppermute | solution.py:43
  10.8 0.0 copy-start.4
  10.8 0.9 %copy-done.4 = bf16[1,48,1024]{2,1,0:T(8,128)(2,1)S(1)} copy-done((bf16[1,48,1024]{2,1,0:T(8,128)(2,1)S(1)}, bf16[1,48,1024]{2,1,0:T(8,128)(2,1)}, u32[]{:S(2)}) %copy-start.4) | copy-done | bytes 98328
  11.7 0.5 group_bank.1.h0
  12.2 0.0 copy-start
  12.2 2.3 %collective-permute-start.6 = (bf16[4,48,1024]{2,1,0:T(8,128)(2,1)S(1)}, bf16[4,48,1024]{2,1,0:T(8,128)(2,1)S(1)}, u32[]{:S(2)}, u32[]{:S(2)}) collective-permute-start(bf16[4,48,1024]{2,1,0:T(8,128)(2,1)S(1)} %group_bank.1.h0), channel_id=1, source_target_pairs={{0,24},{1,7},{2,26},{3,1},{4,28},{5,3},{6,30},{7,5},{8,0},{9,15},{... | collective-permute-start | bytes 1179656 | tf_op jit(solution)/shard_map/ppermute | solution.py:43
  14.5 0.5 collective-permute-start.5
  15.0 0.6 collective-permute-start.4
  15.6 1.5 %broadcast_in_dim.3 = f32[32,2,1024]{2,1,0:T(2,128)} broadcast(f32[2,1024]{1,0:T(2,128)} %bitcast.20), dimensions={1,2} | broadcast | bytes 270336 | tf_op jit(solution)/shard_map/broadcast_in_dim | solution.py:29
  17.1 7.0 %all-to-all-start = ((f32[32,2,1024]{2,1,0:T(2,128)}), f32[32,2,1024]{2,1,0:T(2,128)S(1)}, u32[]{:S(2)}, u32[]{:S(2)}) async-start(f32[32,2,1024]{2,1,0:T(2,128)} %broadcast_in_dim.3), calls=%async_computation | async-start | bytes 524288 | tf_op jit(solution)/shard_map/all_to_all | solution.py:30
  24.0 0.3 collective-permute-start
  25.8 0.1 stack.29.place
  25.8 0.0 copy-start.6
  25.8 0.1 pad_maximum_fusion.factors
  25.9 7.0 %all-to-all-done.rows = f32[32,2,1024]{2,1,0:T(2,128)S(1)} async-done(((f32[32,2,1024]{2,1,0:T(2,128)}), f32[32,2,1024]{2,1,0:T(2,128)S(1)}, u32[]{:S(2)}, u32[]{:S(2)}) %all-to-all-start) | async-done | bytes 262176 | tf_op jit(solution)/shard_map/all_to_all | solution.py:30
  32.9 0.0 copy-start.8
  32.9 0.7 copy-done.8
  33.6 0.0 copy-start.9
  33.6 0.7 copy-done.9
  34.3 10.1 %covariance.1 = (bf16[4,1024,1024]{2,1,0:T(8,128)(2,1)}, f32[4,8,128]{2,1,0:T(8,128)S(1)}, f32[1,2,128]{2,1,0:T(2,128)S(1)}) custom-call(s32[5]{0:T(128)S(1)} %stack.29.place, s32[1]{0:T(128)S(6)} %copy.13.order, f32[2]{0:T(128)S(1)} %pad_maximum_fusion.factors, s32[4]{0:T(128)S(1)} %bitcast.23, f32[32,2,1024]{2,1,0:T(2,128)S(1)} %all-to-all-done.rows, ...), custom_call_target="tpu_custom_call" | custom-call | flops 100000000 | bytes 8388608 | tf_op jit(solution)/shard_map/covariance/pallas_call | solution.py:342
  44.4 0.0 collective-permute-done.their_ids
  44.4 0.0 collective-permute-done.6.h3
  44.4 0.0 copy-start.1
  44.4 0.0 collective-permute-done.5.h2
  44.4 0.0 copy-start.2
  44.4 0.0 collective-permute-done.4.h1
  44.4 0.0 copy-start.3
  44.4 1.6 %select.1 = (bf16[4,48,1024]{2,1,0:T(8,128)(2,1)S(1)}, f32[256,2,128]{2,1,0:T(2,128)}) custom-call(s32[5]{0:T(128)S(1)} %stack.29.place, s32[4]{0:T(128)S(1)} %collective-permute-done.their_ids, f32[1,2,128]{2,1,0:T(2,128)S(1)} %get-tuple-element.15.share, bf16[4,48,1024]{2,1,0:T(8,128)(2,1)S(1)} %group_bank.1.h0, ...), custom_call_target="tpu_custom_call" | custom-call | tf_op jit(solution)/shard_map/select/pallas_call | solution.py:420
  46.1 0.0 copy-done
  46.1 0.0 copy-done.6
  46.1 0.0 copy-start.7
  46.1 3.1 %collective-permute-start.7 = (bf16[4,48,1024]{2,1,0:T(8,128)(2,1)S(1)}, bf16[4,48,1024]{2,1,0:T(8,128)(2,1)S(1)}, u32[]{:S(2)}, u32[]{:S(2)}) collective-permute-start(bf16[4,48,1024]{2,1,0:T(8,128)(2,1)S(1)} %get-tuple-element.16), channel_id=1, source_target_pairs={{0,1},{1,0},{2,3},{3,2},{4,5},{5,4},{6,7},{7,6},{8,9},{9,8},{10,11... | collective-permute-start | bytes 1179656 | tf_op jit(solution)/shard_map/ppermute | solution.py:83
  49.3 9.9 %all-to-all-start.1 = ((f32[256,2,128]{2,1,0:T(2,128)}), f32[256,2,128]{2,1,0:T(2,128)S(1)}, u32[]{:S(2)}, u32[]{:S(2)}) async-start(f32[256,2,128]{2,1,0:T(2,128)} %get-tuple-element.19), calls=%async_computation.1 | async-start | bytes 524288 | tf_op jit(solution)/shard_map/all_to_all | solution.py:430
  59.2 0.0 collective-permute-done.7.got
  59.2 0.0 copy-start.10
  59.2 0.0 copy-done.1
  59.2 0.0 copy-done.2
  59.2 0.0 copy-done.3
  59.2 0.7 copy-done.10
  60.0 14.0 %compress.1 = (f32[4,48,1024]{2,1,0:T(8,128)}, f32[4,48,1024]{2,1,0:T(8,128)}, f32[4,8,128]{2,1,0:T(8,128)}) custom-call(s32[5]{0:T(128)} %copy-done.6, s32[4]{0:T(128)} %bitcast.25, s32[4]{0:T(128)} %bitcast.22, bf16[4,1024,1024]{2,1,0:T(8,128)(2,1)} %get-tuple-element.14.low_hbm, bf16[4,48,1024]{2,1,0:T(8,128)(2,1)} %copy-done.10, ...), custom_call_target="tpu_custom_call" | custom-call | flops 2000000000 | bytes 8388608 | tf_op jit(solution)/shard_map/compress/pallas_call | solution.py:369
  74.0 0.5 all-to-all-done.1.total
  74.6 0.0 copy-done.7
  74.6 0.0 copy-start.5
  74.6 0.7 copy-done.5
  75.3 1.5 %errors.1 = (f32[1,4]{1,0:T(1,128)}, s32[1]{0:T(128)}) custom-call(s32[5]{0:T(128)S(1)} %copy-done.7, f32[256,2,128]{2,1,0:T(2,128)S(1)} %all-to-all-done.1.total, f32[4,8,128]{2,1,0:T(8,128)S(1)} %get-tuple-element.20.norms, f32[4,8,128]{2,1,0:T(8,128)S(1)} %copy-done.5), custom_call_target="tpu_custom_call" | custom-call | tf_op jit(solution)/shard_map/errors/pallas_call | solution.py:434
Async XLA Ops:
  0.6 6.6 %collective-permute-start.3 = (bf16[48,1024]{1,0:T(8,128)(2,1)}, bf16[48,1024]{1,0:T(8,128)(2,1)S(1)}, u32[]{:S(2)}, u32[]{:S(2)}) collective-permute-start(bf16[48,1024]{1,0:T(8,128)(2,1)} %bitcast.16), channel_id=1, source_target_pairs={{0,6},{1,25},{2,0},{3,27},{4,2},{5,29},{6,4},{7,31},{8,14},{9,1},{... | collective-permute-start | bytes 294920 | tf_op jit(solution)/shard_map/ppermute | solution.py:43
  4.3 5.3 %collective-permute-start.2 = (bf16[48,1024]{1,0:T(8,128)(2,1)}, bf16[48,1024]{1,0:T(8,128)(2,1)S(1)}, u32[]{:S(2)}, u32[]{:S(2)}) collective-permute-start(bf16[48,1024]{1,0:T(8,128)(2,1)} %bitcast.17), channel_id=1, source_target_pairs={{0,4},{1,17},{2,6},{3,19},{4,0},{5,21},{6,2},{7,23},{8,12},{9,25},... | collective-permute-start | bytes 294920 | tf_op jit(solution)/shard_map/ppermute | solution.py:43
  4.6 6.2 %collective-permute-start.1 = (bf16[48,1024]{1,0:T(8,128)(2,1)}, bf16[48,1024]{1,0:T(8,128)(2,1)S(1)}, u32[]{:S(2)}, u32[]{:S(2)}) collective-permute-start(bf16[48,1024]{1,0:T(8,128)(2,1)} %bitcast.18), channel_id=1, source_target_pairs={{0,2},{1,9},{2,4},{3,11},{4,6},{5,13},{6,0},{7,15},{8,10},{9,17},{... | collective-permute-start | bytes 294920 | tf_op jit(solution)/shard_map/ppermute | solution.py:43
  10.8 0.9 %copy-start.4 = (bf16[1,48,1024]{2,1,0:T(8,128)(2,1)S(1)}, bf16[1,48,1024]{2,1,0:T(8,128)(2,1)}, u32[]{:S(2)}) copy-start(bf16[1,48,1024]{2,1,0:T(8,128)(2,1)} %param.9) | copy-start | bytes 294916
  12.2 33.9 %copy-start = (bf16[4,48,1024]{2,1,0:T(8,128)(2,1)}, bf16[4,48,1024]{2,1,0:T(8,128)(2,1)S(1)}, u32[]{:S(2)}) copy-start(bf16[4,48,1024]{2,1,0:T(8,128)(2,1)S(1)} %group_bank.1.h0) | copy-start | bytes 1179652
  12.2 32.2 %collective-permute-start.6 = (bf16[4,48,1024]{2,1,0:T(8,128)(2,1)S(1)}, bf16[4,48,1024]{2,1,0:T(8,128)(2,1)S(1)}, u32[]{:S(2)}, u32[]{:S(2)}) collective-permute-start(bf16[4,48,1024]{2,1,0:T(8,128)(2,1)S(1)} %group_bank.1.h0), channel_id=1, source_target_pairs={{0,24},{1,7},{2,26},{3,1},{4,28},{5,3},{6,30},{7,5},{8,0},{9,15},{... | collective-permute-start | bytes 1179656 | tf_op jit(solution)/shard_map/ppermute | solution.py:43
  14.5 29.9 %collective-permute-start.5 = (bf16[4,48,1024]{2,1,0:T(8,128)(2,1)S(1)}, bf16[4,48,1024]{2,1,0:T(8,128)(2,1)S(1)}, u32[]{:S(2)}, u32[]{:S(2)}) collective-permute-start(bf16[4,48,1024]{2,1,0:T(8,128)(2,1)S(1)} %group_bank.1.h0), channel_id=1, source_target_pairs={{0,16},{1,5},{2,18},{3,7},{4,20},{5,1},{6,22},{7,3},{8,24},{9,13},... | collective-permute-start | bytes 1179656 | tf_op jit(solution)/shard_map/ppermute | solution.py:43
  15.0 29.4 %collective-permute-start.4 = (bf16[4,48,1024]{2,1,0:T(8,128)(2,1)S(1)}, bf16[4,48,1024]{2,1,0:T(8,128)(2,1)S(1)}, u32[]{:S(2)}, u32[]{:S(2)}) collective-permute-start(bf16[4,48,1024]{2,1,0:T(8,128)(2,1)S(1)} %group_bank.1.h0), channel_id=1, source_target_pairs={{0,8},{1,3},{2,10},{3,5},{4,12},{5,7},{6,14},{7,1},{8,16},{9,11},{... | collective-permute-start | bytes 1179656 | tf_op jit(solution)/shard_map/ppermute | solution.py:43
  17.1 15.8 %all-to-all-start = ((f32[32,2,1024]{2,1,0:T(2,128)}), f32[32,2,1024]{2,1,0:T(2,128)S(1)}, u32[]{:S(2)}, u32[]{:S(2)}) async-start(f32[32,2,1024]{2,1,0:T(2,128)} %broadcast_in_dim.3), calls=%async_computation | async-start | bytes 524288 | tf_op jit(solution)/shard_map/all_to_all | solution.py:30
  24.0 20.3 %collective-permute-start = (s32[4]{0:T(128)}, s32[4]{0:T(128)S(1)}, u32[]{:S(2)}, u32[]{:S(2)}) collective-permute-start(s32[4]{0:T(128)} %bitcast.24), channel_id=1, source_target_pairs={{0,1},{1,0},{2,3},{3,2},{4,5},{5,4},{6,7},{7,6},{8,9},{9,8},{10,11... | collective-permute-start | bytes 56 | tf_op jit(solution)/shard_map/ppermute | solution.py:83
  25.8 20.3 %copy-start.6 = (s32[5]{0:T(128)}, s32[5]{0:T(128)S(1)}, u32[]{:S(2)}) copy-start(s32[5]{0:T(128)S(1)} %stack.29.place) | copy-start | bytes 64
  32.9 0.7 copy-start.8
  33.6 0.7 copy-start.9
  44.4 14.8 %copy-start.1 = (bf16[4,48,1024]{2,1,0:T(8,128)(2,1)}, bf16[4,48,1024]{2,1,0:T(8,128)(2,1)S(1)}, u32[]{:S(2)}) copy-start(bf16[4,48,1024]{2,1,0:T(8,128)(2,1)S(1)} %collective-permute-done.6.h3) | copy-start | bytes 1179652
  44.4 14.8 %copy-start.2 = (bf16[4,48,1024]{2,1,0:T(8,128)(2,1)}, bf16[4,48,1024]{2,1,0:T(8,128)(2,1)S(1)}, u32[]{:S(2)}) copy-start(bf16[4,48,1024]{2,1,0:T(8,128)(2,1)S(1)} %collective-permute-done.5.h2) | copy-start | bytes 1179652
  44.4 14.8 %copy-start.3 = (bf16[4,48,1024]{2,1,0:T(8,128)(2,1)}, bf16[4,48,1024]{2,1,0:T(8,128)(2,1)S(1)}, u32[]{:S(2)}) copy-start(bf16[4,48,1024]{2,1,0:T(8,128)(2,1)S(1)} %collective-permute-done.4.h1) | copy-start | bytes 1179652
  46.1 28.4 %copy-start.7 = (s32[5]{0:T(128)S(1)}, s32[5]{0:T(128)}, u32[]{:S(2)}) copy-start(s32[5]{0:T(128)} %copy-done.6) | copy-start | bytes 64
  46.1 13.1 %collective-permute-start.7 = (bf16[4,48,1024]{2,1,0:T(8,128)(2,1)S(1)}, bf16[4,48,1024]{2,1,0:T(8,128)(2,1)S(1)}, u32[]{:S(2)}, u32[]{:S(2)}) collective-permute-start(bf16[4,48,1024]{2,1,0:T(8,128)(2,1)S(1)} %get-tuple-element.16), channel_id=1, source_target_pairs={{0,1},{1,0},{2,3},{3,2},{4,5},{5,4},{6,7},{7,6},{8,9},{9,8},{10,11... | collective-permute-start | bytes 1179656 | tf_op jit(solution)/shard_map/ppermute | solution.py:83
  49.3 25.3 %all-to-all-start.1 = ((f32[256,2,128]{2,1,0:T(2,128)}), f32[256,2,128]{2,1,0:T(2,128)S(1)}, u32[]{:S(2)}, u32[]{:S(2)}) async-start(f32[256,2,128]{2,1,0:T(2,128)} %get-tuple-element.19), calls=%async_computation.1 | async-start | bytes 524288 | tf_op jit(solution)/shard_map/all_to_all | solution.py:430
  59.2 0.8 %copy-start.10 = (bf16[4,48,1024]{2,1,0:T(8,128)(2,1)}, bf16[4,48,1024]{2,1,0:T(8,128)(2,1)S(1)}, u32[]{:S(2)}) copy-start(bf16[4,48,1024]{2,1,0:T(8,128)(2,1)S(1)} %collective-permute-done.7.got) | copy-start | bytes 1179652
  74.6 0.7 copy-start.5

commit v3 on v2

--- a/solution.py
+++ b/solution.py
@@ -66,8 +66,8 @@
     return [group] + [plane_shift(group, shift, 1) for shift in (1, 2, 3)]
 
 
-def fetch_entry(place, entry, wanted, held, out, sem, act):
-    c, y, x = place[2], place[3], place[4]
+def fetch_entry(entry, wanted, held, out, sem, act):
+    _, _, c, y, x = position()
     dy = (y - (entry >> 3)) & 3
     dx = (x - ((entry >> 1) & 3)) & 3
     inner = jnp.where(c == 0, dx, dy)
@@ -83,10 +83,21 @@
     return lax.ppermute(value, "pcol_2", [(0, 1), (1, 0)])
 
 
-def covariance_kernel(place, order, factors, ranks, rows, cols, low_hbm, norms, share, low, turned, xb, yb, sems):
-    p, q = place[0], place[1]
-    scale = factors[0]
-    square = factors[1] * scale * scale
+def position():
+    y, x, c = (lax.axis_index(name) for name in PCOL)
+    return lax.axis_index("prow"), (y * 4 + x) * 2 + c, c, y, x
+
+
+def covariance_kernel(
+    order, reach, ranks_hbm, rows, low_hbm, norms, share, low, turned, xb, yb, sems, ranks, ranks_sem
+):
+    bring = pltpu.make_async_copy(ranks_hbm, ranks, ranks_sem)
+    bring.start()
+    p, q, *_unused = position()
+    wide = (16, 128)
+    twice = jnp.full(wide, 2.0 * order[0].astype(jnp.float32) + 1.0, jnp.float32)
+    scale = jnp.sqrt(twice) / jnp.full(wide, reach[0], jnp.float32)
+    square = scale * scale * (1.0 / 3.0)
     power = scale * (-LOG2E)
 
     def tile(k, poly):
@@ -105,8 +116,8 @@
             yr = yb[at, :]
             for n in range(8):
                 lanes = slice(n * 128, (n + 1) * 128)
-                dx = xr - cols[0:1, lanes]
-                dy = yr - cols[1:2, lanes]
+                dx = xr - rows[q, 0:1, lanes]
+                dy = yr - rows[q, 1:2, lanes]
                 d2 = dx * dx + dy * dy
                 r = d2 * lax.rsqrt(jnp.maximum(d2, 1e-30))
                 v = poly(r, jnp.exp2(power * r))
@@ -123,8 +134,7 @@
         lambda r, e: (1.0 + r * (scale + square * r)) * e,
     )
 
-    def slot(k, carry):
-        rank_sum, acc = carry
+    def slot(k, acc):
         i = k * 8 + p
         norms[k] = jnp.zeros((8, 128), jnp.float32)
         for which in range(3):
@@ -138,32 +148,31 @@
             pltpu.make_async_copy(low.at[k], low_hbm.at[k], sems.at[k]).start()
 
         acc = acc + jnp.where(q < i, 2.0, 1.0) * norms[k]
-        return rank_sum + jnp.where(q < i, ranks[k], 0), acc
-
-    rank_sum, acc = lax.fori_loop(
-        0, SLOTS, slot, (jnp.int32(0), jnp.zeros((8, 128), jnp.float32))
-    )
+        return acc
+
+    acc = lax.fori_loop(0, SLOTS, slot, jnp.zeros((8, 128), jnp.float32))
+    bring.wait()
+    rank_sum = jnp.int32(0)
+    for k in range(SLOTS):
+        rank_sum = rank_sum + jnp.where(q < k * 8 + p, ranks[k], 0)
     for k in range(SLOTS):
 
         @pl.when(q <= k * 8 + p)
         def _(k=k):
             pltpu.make_async_copy(low.at[k], low_hbm.at[k], sems.at[k]).wait()
 
-    acc = jnp.sum(acc, axis=0, keepdims=True)
+    acc = jnp.sum(jnp.sum(acc, axis=0, keepdims=True), axis=1, keepdims=True)
     lane = lax.broadcasted_iota(jnp.int32, (1, 128), 1)
-    both = jnp.concatenate([acc, jnp.where(lane == 0, rank_sum.astype(jnp.float32), 0.0)], 0)
-    share[...] = both[None]
-
-
-def select_kernel(place, their_ids, share, h0, h1, h2, h3, theirs, again, sems):
+    both = jnp.where(lane == 0, acc, jnp.where(lane == 1, rank_sum.astype(jnp.float32), 0.0))
+    share[...] = jnp.broadcast_to(both[None], share.shape)
+
+
+def select_kernel(their_ids, h0, h1, h2, h3, theirs, sems):
     def each(act):
         for k in range(SLOTS):
-            fetch_entry(
-                place, their_ids[k], True, (h0, h1, h2, h3), theirs.at[k], sems.at[k], act
-            )
+            fetch_entry(their_ids[k], True, (h0, h1, h2, h3), theirs.at[k], sems.at[k], act)
 
     each(lambda copy: copy.start())
-    again[...] = jnp.broadcast_to(share[...], again.shape)
     each(lambda copy: copy.wait())
 
 
@@ -225,10 +234,10 @@
 
 
 def compress_kernel(
-    place, ids, ranks, low_hbm, got, h0, h1, h2, h3, y_out, c_out, err_out,
+    ids, ranks, norms, low_hbm, got, h0, h1, h2, h3, y_out, c_out, err_out,
     low, sk, w_all, h_all, zt, cz, sems, low_sems,
 ):
-    p, q, c = place[0], place[1], place[2]
+    p, q, c, *_unused = position()
     dot = functools.partial(jnp.dot, preferred_element_type=jnp.float32)
 
     def slot_of(k):
@@ -239,7 +248,7 @@
             a, active = slot_of(k)
             e = ids[a]
 
-            fetch_entry(place, e, active, (h0, h1, h2, h3), sk.at[k], sems.at[k], act)
+            fetch_entry(e, active, (h0, h1, h2, h3), sk.at[k], sems.at[k], act)
 
             @pl.when(active & ((e & 1) != c))
             def _(k=k, a=a):
@@ -299,7 +308,7 @@
 
     for k in range(SLOTS):
         a, active = slot_of(k)
-        err_out[k] = jnp.zeros((8, 128), jnp.float32)
+        err_out[k] = jnp.where(q == k * 8 + p, norms[k], 0.0)
 
         @pl.when(active)
         def _(k=k, a=a):
@@ -321,19 +330,17 @@
             err_out[k] = acc
 
 
-def error_kernel(place, total, norms, errs, out, rank_out):
-    p, q = place[0], place[1]
+def error_kernel(total, errs, out, rank_out):
     summed = jnp.sum(total[...], axis=0)
-    whole = jnp.sum(summed[0:1, :])
+    whole = summed[:, 0:1]
     lane = lax.broadcasted_iota(jnp.int32, (1, 128), 1)
     values = jnp.zeros((1, 128), jnp.float32)
     for k in range(SLOTS):
-        i = k * 8 + p
-        kept = jnp.where(q < i, jnp.sum(errs[k]), jnp.where(q == i, jnp.sum(norms[k]), 0.0))
+        kept = jnp.sum(jnp.sum(errs[k], axis=0, keepdims=True), axis=1, keepdims=True)
         values = jnp.where(lane == k, kept, values)
-    result = 32.0 * jnp.sqrt(values) / jnp.sqrt(jnp.full((1, 128), whole, jnp.float32))
+    result = 32.0 * jnp.sqrt(values) / jnp.sqrt(whole)
     out[...] = result[:, :SLOTS]
-    rank_out[0] = jnp.sum(summed[1:2, :]).astype(jnp.int32)
+    rank_out[0] = jnp.sum(summed[:, 1:2]).astype(jnp.int32)
 
 
 def covariance(*args):
@@ -344,9 +351,9 @@
         out_shape=(
             shape((SLOTS, TILE, TILE), bf16),
             shape((SLOTS, 8, 128), f32),
-            shape((1, 2, 128), f32),
+            shape((256, 1, 128), f32),
         ),
-        in_specs=[spec(SMEM)] * 4 + [spec(VMEM)] * 2,
+        in_specs=[spec(SMEM)] * 2 + [spec(pltpu.HBM), spec(VMEM)],
         out_specs=[spec(pltpu.HBM)] + [spec(VMEM)] * 2,
         scratch_shapes=[
             VMEM((SLOTS, TILE, TILE), bf16),
@@ -354,6 +361,8 @@
             VMEM((TILE, 128), f32),
             VMEM((TILE, 128), f32),
             pltpu.SemaphoreType.DMA((SLOTS,)),
+            SMEM((SLOTS,), jnp.int32),
+            pltpu.SemaphoreType.DMA,
         ],
         compiler_params=pltpu.CompilerParams(vmem_limit_bytes=50 << 20),
         cost_estimate=pl.CostEstimate(
@@ -373,7 +382,7 @@
             shape((SLOTS, RANKS, TILE), f32),
             shape((SLOTS, 8, 128), f32),
         ),
-        in_specs=[spec(SMEM)] * 3 + [spec(pltpu.HBM)] + [spec(pl.ANY)] * 5,
+        in_specs=[spec(SMEM)] * 2 + [spec(VMEM)] + [spec(pltpu.HBM), spec(VMEM)] + [spec(pl.ANY)] * 4,
         out_specs=[spec(VMEM)] * 3,
         scratch_shapes=[
             VMEM((SLOTS, TILE, TILE), bf16),
@@ -385,7 +394,7 @@
             pltpu.SemaphoreType.DMA((SLOTS,)),
             pltpu.SemaphoreType.DMA((SLOTS, PARTS)),
         ],
-        compiler_params=pltpu.CompilerParams(vmem_limit_bytes=60 << 20),
+        compiler_params=pltpu.CompilerParams(vmem_limit_bytes=50 << 20),
         cost_estimate=pl.CostEstimate(
             flops=2_000_000_000, bytes_accessed=8 << 20, transcendentals=0
         ),
@@ -396,49 +405,38 @@
 def device_program(points, range_length, smoothness, sketch_bank, sketch_ids, tile_ranks):
     f32, bf16, i32 = jnp.float32, jnp.bfloat16, jnp.int32
     shape = jax.ShapeDtypeStruct
-    p = lax.axis_index("prow")
-    y, x, c = (lax.axis_index(n) for n in PCOL)
-    place = jnp.stack([p, (y * 4 + x) * 2 + c, c, y, x]).astype(i32)
-    s = smoothness[0]
-    factors = jnp.stack(
-        [
-            jnp.sqrt(2.0 * s.astype(f32) + 1.0) / range_length[0],
-            jnp.float32(1.0 / 3.0),
-        ]
-    )
     ids = sketch_ids.reshape(SLOTS)
     ranks = tile_ranks.reshape(SLOTS)
     own = points.reshape(2, TILE)
 
-    order = smoothness.astype(i32)
     rows = to_all(own, PCOL)
     held = bank_of_plane(sketch_bank[0])
     their_ids = swap_cores(ids)
 
-    low, norms, share = covariance(place, order, factors, ranks, rows, own)
-
-    theirs, again = pl.pallas_call(
+    low, norms, share = covariance(smoothness, range_length, ranks, rows)
+
+    theirs = pl.pallas_call(
         select_kernel,
-        out_shape=(shape((SLOTS, RANKS, TILE), bf16), shape((256, 2, 128), f32)),
-        in_specs=[spec(SMEM)] * 2 + [spec(VMEM)] + [spec(pl.ANY)] * 4,
-        out_specs=[spec(VMEM)] * 2,
+        out_shape=shape((SLOTS, RANKS, TILE), bf16),
+        in_specs=[spec(SMEM)] + [spec(pl.ANY)] * 4,
+        out_specs=spec(VMEM),
         scratch_shapes=[pltpu.SemaphoreType.DMA((SLOTS,))],
         compiler_params=pltpu.CompilerParams(vmem_limit_bytes=4 << 20),
         name="select",
-    )(place, their_ids, share, *held)
+    )(their_ids, *held)
     got = swap_cores(theirs)
-    total = lax.all_to_all(again, ALL, split_axis=0, concat_axis=0)
-
-    y_all, c_all, errs = compress(place, ids, ranks, low, got, *held)
+    total = lax.all_to_all(share, ALL, split_axis=0, concat_axis=0)
+
+    y_all, c_all, errs = compress(ids, ranks, norms, low, got, *held)
 
     errors, rank_out = pl.pallas_call(
         error_kernel,
         out_shape=(shape((1, SLOTS), f32), shape((1,), i32)),
-        in_specs=[spec(SMEM)] + [spec(VMEM)] * 3,
+        in_specs=[spec(VMEM)] * 2,
         out_specs=[spec(VMEM), spec(SMEM)],
         compiler_params=pltpu.CompilerParams(vmem_limit_bytes=4 << 20),
         name="errors",
-    )(place, total, norms, errs)
+    )(total, errs)
 
     wide = (SLOTS, 1, 1, 1, RANKS, TILE)
     return (

time: 77.4 us -> 85.5 us (1.10); the launches traced: 76.9 us -> 83.8 us
  waiting for transfers between devices: 13 us -> 21.7 us
  local copies, waits for them, and re-layouts: 5.28 us -> 3.02 us
  starting transfers between devices: 28.4 us -> 30.6 us
  Pallas kernels: 27.7 us -> 26.3 us
    ppermute x6, waiting for transfers between devices: 5.5 us -> 13.2 us  [plane_shift(): return lax.ppermute(value, PCOL, pairs)]
    all_to_all x1, starting transfers between devices: 6.96 us -> 3.79 us  [to_all(): return lax.all_to_all(copies, axes, split_axis=0, concat_axis=0)]
    ppermute x2, starting transfers between devices: 3.46 us -> 6.43 us  [swap_cores(): return lax.ppermute(value, 'pcol_2', [(0, 1), (1, 0)])]
    all_to_all x1, starting transfers between devices: 9.91 us -> 12.3 us  [device_program(): total = lax.all_to_all(share, ALL, split_axis=0, concat_axis=0)]
    unnamed x22 -> x8, local copies, waits for them, and re-layouts: 3.73 us -> 1.56 us
    ppermute x2, waiting for transfers between devices: 0.01 us -> 0.96 us  [swap_cores(): return lax.ppermute(value, 'pcol_2', [(0, 1), (1, 0)])]
  transfers between devices with their start and end apart: 10 -> 10, of which waited for: 5 -> 7; matrix products, arithmetic and copies ran while one was open for 2% -> 2% of each run, Pallas kernels for 31% -> 29%
where the time goes in v3:
time: 85.5 us; the launch traced here: 83.8 us
  starting transfers between devices  30.6 us (36%)
  Pallas kernels  26.3 us (31%)
  waiting for transfers between devices  21.7 us (25%)
  local copies, waits for them, and re-layouts  3.02 us (4%)
  between operations  2.18 us (3%)
    pallas_call x1, Pallas kernels, compress(): pl.pallas_call(compress_kernel, out_shape=(shape((SLOTS, RANKS, TILE), f3...  13.5 us
    ppermute x6, waiting for transfers between devices, plane_shift(): return lax.ppermute(value, PCOL, pairs)  13.2 us
    all_to_all x1, starting transfers between devices, device_program(): total = lax.all_to_all(share, ALL, split_axis=0, concat_axis=0)  12.3 us
    pallas_call x1, Pallas kernels, covariance(): pl.pallas_call(covariance_kernel, out_shape=(shape((SLOTS, TILE, TILE), b...  10.5 us
    ppermute x6, starting transfers between devices, plane_shift(): return lax.ppermute(value, PCOL, pairs)  8.06 us
    all_to_all x1, waiting for transfers between devices, to_all(): return lax.all_to_all(copies, axes, split_axis=0, concat_axis=0)  7.57 us
    ppermute x2, starting transfers between devices, swap_cores(): return lax.ppermute(value, 'pcol_2', [(0, 1), (1, 0)])  6.43 us
    all_to_all x1, starting transfers between devices, to_all(): return lax.all_to_all(copies, axes, split_axis=0, concat_axis=0)  3.79 us
  transfers between devices with their start and end apart: 10, of which 7 were waited for; matrix products, arithmetic and copies ran while one was open for 2% of the time, Pallas kernels for 29%

profile of v3, /device:TPU:1, one launch (start us, length us, event | category | flops | bytes accessed | tf_op | source)
XLA Modules:
  0.0 83.8 jit_solution(3329053792228456000)
XLA Ops:
  0.6 3.6 %collective-permute-start.3 = (bf16[48,1024]{1,0:T(8,128)(2,1)}, bf16[48,1024]{1,0:T(8,128)(2,1)S(1)}, u32[]{:S(2)}, u32[]{:S(2)}) collective-permute-start(bf16[48,1024]{1,0:T(8,128)(2,1)} %bitcast.11), channel_id=1, source_target_pairs={{0,6},{1,25},{2,0},{3,27},{4,2},{5,29},{6,4},{7,31},{8,14},{9,1},{... | collective-permute-start | bytes 294920 | tf_op jit(solution)/shard_map/ppermute | solution.py:43
  4.3 0.3 collective-permute-start.2
  4.6 0.7 collective-permute-start.1
  5.3 1.9 %collective-permute-done.3.refs_3_ = bf16[48,1024]{1,0:T(8,128)(2,1)S(1)} collective-permute-done((bf16[48,1024]{1,0:T(8,128)(2,1)}, bf16[48,1024]{1,0:T(8,128)(2,1)S(1)}, u32[]{:S(2)}, u32[]{:S(2)}) %collective-permute-start.3) | collective-permute-done | bytes 98336 | tf_op jit(solution)/shard_map/ppermute | solution.py:43
  7.2 2.3 %collective-permute-done.2.refs_2_ = bf16[48,1024]{1,0:T(8,128)(2,1)S(1)} collective-permute-done((bf16[48,1024]{1,0:T(8,128)(2,1)}, bf16[48,1024]{1,0:T(8,128)(2,1)S(1)}, u32[]{:S(2)}, u32[]{:S(2)}) %collective-permute-start.2) | collective-permute-done | bytes 98336 | tf_op jit(solution)/shard_map/ppermute | solution.py:43
  9.5 1.2 %collective-permute-done.1.refs_1_ = bf16[48,1024]{1,0:T(8,128)(2,1)S(1)} collective-permute-done((bf16[48,1024]{1,0:T(8,128)(2,1)}, bf16[48,1024]{1,0:T(8,128)(2,1)S(1)}, u32[]{:S(2)}, u32[]{:S(2)}) %collective-permute-start.1) | collective-permute-done | bytes 98336 | tf_op jit(solution)/shard_map/ppermute | solution.py:43
  10.8 0.0 copy-start
  10.8 0.9 %copy-done = bf16[1,48,1024]{2,1,0:T(8,128)(2,1)S(1)} copy-done((bf16[1,48,1024]{2,1,0:T(8,128)(2,1)S(1)}, bf16[1,48,1024]{2,1,0:T(8,128)(2,1)}, u32[]{:S(2)}) %copy-start) | copy-done | bytes 98328
  11.7 0.5 group_bank.1.h0
  12.2 2.3 %collective-permute-start.6 = (bf16[4,48,1024]{2,1,0:T(8,128)(2,1)S(1)}, bf16[4,48,1024]{2,1,0:T(8,128)(2,1)S(1)}, u32[]{:S(2)}, u32[]{:S(2)}) collective-permute-start(bf16[4,48,1024]{2,1,0:T(8,128)(2,1)S(1)} %group_bank.1.h0), channel_id=1, source_target_pairs={{0,24},{1,7},{2,26},{3,1},{4,28},{5,3},{6,30},{7,5},{8,0},{9,15},{... | collective-permute-start | bytes 1179656 | tf_op jit(solution)/shard_map/ppermute | solution.py:43
  14.5 0.5 collective-permute-start.5
  15.0 0.6 collective-permute-start.4
  15.6 2.9 %collective-permute-start = (s32[4]{0:T(128)}, s32[4]{0:T(128)S(1)}, u32[]{:S(2)}, u32[]{:S(2)}) collective-permute-start(s32[4]{0:T(128)} %bitcast.15), channel_id=1, source_target_pairs={{0,1},{1,0},{2,3},{3,2},{4,5},{5,4},{6,7},{7,6},{8,9},{9,8},{10,11... | collective-permute-start | bytes 56 | tf_op jit(solution)/shard_map/ppermute | solution.py:83
  18.5 1.0 %collective-permute-done.their_ids = s32[4]{0:T(128)S(1)} collective-permute-done((s32[4]{0:T(128)}, s32[4]{0:T(128)S(1)}, u32[]{:S(2)}, u32[]{:S(2)}) %collective-permute-start) | collective-permute-done | bytes 48 | tf_op jit(solution)/shard_map/ppermute | solution.py:83
  19.4 4.0 %collective-permute-done.6.h3 = bf16[4,48,1024]{2,1,0:T(8,128)(2,1)S(1)} collective-permute-done((bf16[4,48,1024]{2,1,0:T(8,128)(2,1)S(1)}, bf16[4,48,1024]{2,1,0:T(8,128)(2,1)S(1)}, u32[]{:S(2)}, u32[]{:S(2)}) %collective-permute-start.6) | collective-permute-done | bytes 393248 | tf_op jit(solution)/shard_map/ppermute | solution.py:43
  23.4 0.0 collective-permute-done.5.h2
  23.4 3.7 %collective-permute-done.4.h1 = bf16[4,48,1024]{2,1,0:T(8,128)(2,1)S(1)} collective-permute-done((bf16[4,48,1024]{2,1,0:T(8,128)(2,1)S(1)}, bf16[4,48,1024]{2,1,0:T(8,128)(2,1)S(1)}, u32[]{:S(2)}, u32[]{:S(2)}) %collective-permute-start.4) | collective-permute-done | bytes 393248 | tf_op jit(solution)/shard_map/ppermute | solution.py:43
  27.1 0.9 %select.1 = bf16[4,48,1024]{2,1,0:T(8,128)(2,1)S(1)} custom-call(s32[4]{0:T(128)S(1)} %collective-permute-done.their_ids, bf16[4,48,1024]{2,1,0:T(8,128)(2,1)S(1)} %group_bank.1.h0, bf16[4,48,1024]{2,1,0:T(8,128)(2,1)S(1)} %collective-permute-done.4.h1, bf16[4,48,1024]{2,1,0:T(8,128)(2,1)S(1)} %collective-permute-done.5.h2, ...), custom_call_target="tpu_custom_call" | custom-call | tf_op jit(solution)/shard_map/select/pallas_call | solution.py:418
  28.0 3.6 %collective-permute-start.7 = (bf16[4,48,1024]{2,1,0:T(8,128)(2,1)S(1)}, bf16[4,48,1024]{2,1,0:T(8,128)(2,1)S(1)}, u32[]{:S(2)}, u32[]{:S(2)}) collective-permute-start(bf16[4,48,1024]{2,1,0:T(8,128)(2,1)S(1)} %select.1), channel_id=1, source_target_pairs={{0,1},{1,0},{2,3},{3,2},{4,5},{5,4},{6,7},{7,6},{8,9},{9,8},{10,11... | collective-permute-start | bytes 1179656 | tf_op jit(solution)/shard_map/ppermute | solution.py:83
  31.6 1.5 %broadcast_in_dim.3 = f32[32,2,1024]{2,1,0:T(2,128)} broadcast(f32[2,1024]{1,0:T(2,128)} %bitcast.19), dimensions={1,2} | broadcast | bytes 270336 | tf_op jit(solution)/shard_map/broadcast_in_dim | solution.py:29
  33.0 0.0 copy-start.1
  33.0 0.0 copy-start.3
  33.0 3.8 %all-to-all-start = ((f32[32,2,1024]{2,1,0:T(2,128)}), f32[32,2,1024]{2,1,0:T(2,128)S(1)}, u32[]{:S(2)}, u32[]{:S(2)}) async-start(f32[32,2,1024]{2,1,0:T(2,128)} %broadcast_in_dim.3), calls=%async_computation | async-start | bytes 524288 | tf_op jit(solution)/shard_map/all_to_all | solution.py:30
  38.1 7.6 %all-to-all-done.rows = f32[32,2,1024]{2,1,0:T(2,128)S(1)} async-done(((f32[32,2,1024]{2,1,0:T(2,128)}), f32[32,2,1024]{2,1,0:T(2,128)S(1)}, u32[]{:S(2)}, u32[]{:S(2)}) %all-to-all-start) | async-done | bytes 262176 | tf_op jit(solution)/shard_map/all_to_all | solution.py:30
  45.7 0.0 copy-start.2
  45.7 0.7 copy-done.2
  46.4 10.5 %covariance.1 = (bf16[4,1024,1024]{2,1,0:T(8,128)(2,1)}, f32[4,8,128]{2,1,0:T(8,128)S(1)}, f32[256,1,128]{2,1,0:T(1,128)}) custom-call(s32[1]{0:T(128)S(6)} %copy.13.order, f32[1]{0:T(128)S(6)} %copy.12.reach, s32[4]{0:T(128)S(1)} %bitcast.17, f32[32,2,1024]{2,1,0:T(2,128)S(1)} %all-to-all-done.rows), custom_call_target="tpu_custom_call" | custom-call | flops 100000000 | bytes 8388608 | tf_op jit(solution)/shard_map/covariance/pallas_call | solution.py:349
  56.8 12.3 %all-to-all-start.1 = ((f32[256,1,128]{2,1,0:T(1,128)}), f32[256,1,128]{2,1,0:T(1,128)S(1)}, u32[]{:S(2)}, u32[]{:S(2)}) async-start(f32[256,1,128]{2,1,0:T(1,128)} %get-tuple-element.16), calls=%async_computation.1 | async-start | bytes 262144 | tf_op jit(solution)/shard_map/all_to_all | solution.py:428
  69.2 0.0 collective-permute-done.7.got
  69.2 0.0 copy-done.1
  69.2 0.0 copy-done.3
  69.2 13.5 %compress.1 = (f32[4,48,1024]{2,1,0:T(8,128)}, f32[4,48,1024]{2,1,0:T(8,128)}, f32[4,8,128]{2,1,0:T(8,128)S(1)}) custom-call(s32[4]{0:T(128)S(1)} %bitcast.16, s32[4]{0:T(128)S(1)} %bitcast.18, f32[4,8,128]{2,1,0:T(8,128)S(1)} %get-tuple-element.12.norms, bf16[4,1024,1024]{2,1,0:T(8,128)(2,1)} %get-tuple-element.13.low_hbm, ...), custom_call_target="tpu_custom_call" | custom-call | flops 2000000000 | bytes 8388608 | tf_op jit(solution)/shard_map/compress/pallas_call | solution.py:378
  82.7 0.0 all-to-all-done.1.total
  82.7 0.9 %errors.1 = (f32[1,4]{1,0:T(1,128)}, s32[1]{0:T(128)}) custom-call(f32[256,1,128]{2,1,0:T(1,128)S(1)} %all-to-all-done.1.total, f32[4,8,128]{2,1,0:T(8,128)S(1)} %get-tuple-element.17.errs), custom_call_target="tpu_custom_call" | custom-call | tf_op jit(solution)/shard_map/errors/pallas_call | solution.py:432
Async XLA Ops:
  0.6 6.6 %collective-permute-start.3 = (bf16[48,1024]{1,0:T(8,128)(2,1)}, bf16[48,1024]{1,0:T(8,128)(2,1)S(1)}, u32[]{:S(2)}, u32[]{:S(2)}) collective-permute-start(bf16[48,1024]{1,0:T(8,128)(2,1)} %bitcast.11), channel_id=1, source_target_pairs={{0,6},{1,25},{2,0},{3,27},{4,2},{5,29},{6,4},{7,31},{8,14},{9,1},{... | collective-permute-start | bytes 294920 | tf_op jit(solution)/shard_map/ppermute | solution.py:43
  4.3 5.3 %collective-permute-start.2 = (bf16[48,1024]{1,0:T(8,128)(2,1)}, bf16[48,1024]{1,0:T(8,128)(2,1)S(1)}, u32[]{:S(2)}, u32[]{:S(2)}) collective-permute-start(bf16[48,1024]{1,0:T(8,128)(2,1)} %bitcast.12), channel_id=1, source_target_pairs={{0,4},{1,17},{2,6},{3,19},{4,0},{5,21},{6,2},{7,23},{8,12},{9,25},... | collective-permute-start | bytes 294920 | tf_op jit(solution)/shard_map/ppermute | solution.py:43
  4.6 6.2 %collective-permute-start.1 = (bf16[48,1024]{1,0:T(8,128)(2,1)}, bf16[48,1024]{1,0:T(8,128)(2,1)S(1)}, u32[]{:S(2)}, u32[]{:S(2)}) collective-permute-start(bf16[48,1024]{1,0:T(8,128)(2,1)} %bitcast.13), channel_id=1, source_target_pairs={{0,2},{1,9},{2,4},{3,11},{4,6},{5,13},{6,0},{7,15},{8,10},{9,17},{... | collective-permute-start | bytes 294920 | tf_op jit(solution)/shard_map/ppermute | solution.py:43
  10.8 0.9 %copy-start = (bf16[1,48,1024]{2,1,0:T(8,128)(2,1)S(1)}, bf16[1,48,1024]{2,1,0:T(8,128)(2,1)}, u32[]{:S(2)}) copy-start(bf16[1,48,1024]{2,1,0:T(8,128)(2,1)} %param.9) | copy-start | bytes 294916
  12.2 11.2 %collective-permute-start.6 = (bf16[4,48,1024]{2,1,0:T(8,128)(2,1)S(1)}, bf16[4,48,1024]{2,1,0:T(8,128)(2,1)S(1)}, u32[]{:S(2)}, u32[]{:S(2)}) collective-permute-start(bf16[4,48,1024]{2,1,0:T(8,128)(2,1)S(1)} %group_bank.1.h0), channel_id=1, source_target_pairs={{0,24},{1,7},{2,26},{3,1},{4,28},{5,3},{6,30},{7,5},{8,0},{9,15},{... | collective-permute-start | bytes 1179656 | tf_op jit(solution)/shard_map/ppermute | solution.py:43
  14.5 8.9 %collective-permute-start.5 = (bf16[4,48,1024]{2,1,0:T(8,128)(2,1)S(1)}, bf16[4,48,1024]{2,1,0:T(8,128)(2,1)S(1)}, u32[]{:S(2)}, u32[]{:S(2)}) collective-permute-start(bf16[4,48,1024]{2,1,0:T(8,128)(2,1)S(1)} %group_bank.1.h0), channel_id=1, source_target_pairs={{0,16},{1,5},{2,18},{3,7},{4,20},{5,1},{6,22},{7,3},{8,24},{9,13},... | collective-permute-start | bytes 1179656 | tf_op jit(solution)/shard_map/ppermute | solution.py:43
  15.0 12.1 %collective-permute-start.4 = (bf16[4,48,1024]{2,1,0:T(8,128)(2,1)S(1)}, bf16[4,48,1024]{2,1,0:T(8,128)(2,1)S(1)}, u32[]{:S(2)}, u32[]{:S(2)}) collective-permute-start(bf16[4,48,1024]{2,1,0:T(8,128)(2,1)S(1)} %group_bank.1.h0), channel_id=1, source_target_pairs={{0,8},{1,3},{2,10},{3,5},{4,12},{5,7},{6,14},{7,1},{8,16},{9,11},{... | collective-permute-start | bytes 1179656 | tf_op jit(solution)/shard_map/ppermute | solution.py:43
  15.6 3.8 %collective-permute-start = (s32[4]{0:T(128)}, s32[4]{0:T(128)S(1)}, u32[]{:S(2)}, u32[]{:S(2)}) collective-permute-start(s32[4]{0:T(128)} %bitcast.15), channel_id=1, source_target_pairs={{0,1},{1,0},{2,3},{3,2},{4,5},{5,4},{6,7},{7,6},{8,9},{9,8},{10,11... | collective-permute-start | bytes 56 | tf_op jit(solution)/shard_map/ppermute | solution.py:83
  28.0 41.2 %collective-permute-start.7 = (bf16[4,48,1024]{2,1,0:T(8,128)(2,1)S(1)}, bf16[4,48,1024]{2,1,0:T(8,128)(2,1)S(1)}, u32[]{:S(2)}, u32[]{:S(2)}) collective-permute-start(bf16[4,48,1024]{2,1,0:T(8,128)(2,1)S(1)} %select.1), channel_id=1, source_target_pairs={{0,1},{1,0},{2,3},{3,2},{4,5},{5,4},{6,7},{7,6},{8,9},{9,8},{10,11... | collective-permute-start | bytes 1179656 | tf_op jit(solution)/shard_map/ppermute | solution.py:83
  33.0 36.1 %copy-start.1 = (s32[4,1,1,1]{0,3,2,1:T(1,128)S(1)}, s32[4,1,1,1]{0,3,2,1:T(1,128)}, u32[]{:S(2)}) copy-start(s32[4,1,1,1]{0,3,2,1:T(1,128)} %param.10) | copy-start | bytes 52
  33.0 36.2 %copy-start.3 = (s32[4,1,1,1]{0,3,2,1:T(1,128)S(1)}, s32[4,1,1,1]{0,3,2,1:T(1,128)}, u32[]{:S(2)}) copy-start(s32[4,1,1,1]{0,3,2,1:T(1,128)} %param.11) | copy-start | bytes 52
  33.0 12.7 %all-to-all-start = ((f32[32,2,1024]{2,1,0:T(2,128)}), f32[32,2,1024]{2,1,0:T(2,128)S(1)}, u32[]{:S(2)}, u32[]{:S(2)}) async-start(f32[32,2,1024]{2,1,0:T(2,128)} %broadcast_in_dim.3), calls=%async_computation | async-start | bytes 524288 | tf_op jit(solution)/shard_map/all_to_all | solution.py:30
  45.7 0.7 copy-start.2
  56.8 25.9 %all-to-all-start.1 = ((f32[256,1,128]{2,1,0:T(1,128)}), f32[256,1,128]{2,1,0:T(1,128)S(1)}, u32[]{:S(2)}, u32[]{:S(2)}) async-start(f32[256,1,128]{2,1,0:T(1,128)} %get-tuple-element.16), calls=%async_computation.1 | async-start | bytes 262144 | tf_op jit(solution)/shard_map/all_to_all | solution.py:428

commit v4 on v3

--- a/solution.py
+++ b/solution.py
@@ -279,17 +279,30 @@
     for k in range(SLOTS):
         a, active = slot_of(k)
 
-        pl.when(active)(functools.partial(load, k, lambda copy: copy.wait()))
+        if k > 0:
+            pl.when(active)(functools.partial(load, k, lambda copy: copy.wait()))
         if k + 1 < SLOTS:
             ahead = functools.partial(load, k + 1, lambda copy: copy.start())
-            pl.when(slot_of(k + 1)[1])(ahead)
+            later = slot_of(k + 1)[1]
+            pl.when(later & jnp.logical_not(active) if k == 0 else later)(ahead)
 
         @pl.when(active)
         def _(k=k, a=a):
             rank = ranks[a]
             row = lax.broadcasted_iota(jnp.int32, (RANKS, TILE), 0)
             chosen = jnp.where(row < rank, sk[k].astype(jnp.float32), 0.0).astype(jnp.bfloat16)
-            sketched = dot_nt(chosen, low[k])
+            if k == 0:
+                pieces = []
+                for m in range(PARTS):
+                    part = pl.ds(m * (TILE // PARTS), TILE // PARTS)
+                    pltpu.make_async_copy(
+                        low_hbm.at[0, part], low.at[0, part], low_sems.at[0, m]
+                    ).wait()
+                    pieces.append(dot_nt(chosen, low[0, part, :]))
+                load(1, lambda copy: copy.start())
+                sketched = jnp.concatenate(pieces, 1)
+            else:
+                sketched = dot_nt(chosen, low[k])
             y_out[a] = sketched
             parts = split3(sketched)
             w_all[k] = dot(parts[0], low[k])

time: 85.5 us -> 86.3 us (level)
  the two profiles are of different devices: /device:TPU:1 before, /device:TPU:65 now
where the time goes in v4:
time: 86.3 us; the launch traced here: 85.9 us
  Pallas kernels  32.3 us (37%)
  starting transfers between devices  26.7 us (31%)
  waiting for transfers between devices  21.7 us (25%)
  local copies, waits for them, and re-layouts  3.02 us (3%)
  between operations  2.18 us (3%)
    pallas_call x1, Pallas kernels, compress(): pl.pallas_call(compress_kernel, out_shape=(shape((SLOTS, RANKS, TILE), f3...  16.8 us
    pallas_call x1, Pallas kernels, covariance(): pl.pallas_call(covariance_kernel, out_shape=(shape((SLOTS, TILE, TILE), b...  13.2 us
    ppermute x6, waiting for transfers between devices, plane_shift(): return lax.ppermute(value, PCOL, pairs)  13.2 us
    all_to_all x1, starting transfers between devices, device_program(): total = lax.all_to_all(share, ALL, split_axis=0, concat_axis=0)  9.47 us
    all_to_all x1, waiting for transfers between devices, to_all(): return lax.all_to_all(copies, axes, split_axis=0, concat_axis=0)  7.57 us
    ppermute x6, starting transfers between devices, plane_shift(): return lax.ppermute(value, PCOL, pairs)  7.24 us
    ppermute x2, starting transfers between devices, swap_cores(): return lax.ppermute(value, 'pcol_2', [(0, 1), (1, 0)])  6.19 us
    all_to_all x1, starting transfers between devices, to_all(): return lax.all_to_all(copies, axes, split_axis=0, concat_axis=0)  3.79 us
  transfers between devices with their start and end apart: 10, of which 7 were waited for; matrix products, arithmetic and copies ran while one was open for 2% of the time, Pallas kernels for 35%

profile of v4, /device:TPU:65, one launch (start us, length us, event | category | flops | bytes accessed | tf_op | source)
XLA Modules:
  0.0 85.9 jit_solution(7814767782587061597)
XLA Ops:
  0.6 2.8 %collective-permute-start.3 = (bf16[48,1024]{1,0:T(8,128)(2,1)}, bf16[48,1024]{1,0:T(8,128)(2,1)S(1)}, u32[]{:S(2)}, u32[]{:S(2)}) collective-permute-start(bf16[48,1024]{1,0:T(8,128)(2,1)} %bitcast.11), channel_id=1, source_target_pairs={{0,6},{1,25},{2,0},{3,27},{4,2},{5,29},{6,4},{7,31},{8,14},{9,1},{... | collective-permute-start | bytes 294920 | tf_op jit(solution)/shard_map/ppermute | solution.py:43
  3.4 0.3 collective-permute-start.2
  3.8 0.7 collective-permute-start.1
  4.5 1.9 %collective-permute-done.3.refs_3_ = bf16[48,1024]{1,0:T(8,128)(2,1)S(1)} collective-permute-done((bf16[48,1024]{1,0:T(8,128)(2,1)}, bf16[48,1024]{1,0:T(8,128)(2,1)S(1)}, u32[]{:S(2)}, u32[]{:S(2)}) %collective-permute-start.3) | collective-permute-done | bytes 98336 | tf_op jit(solution)/shard_map/ppermute | solution.py:43
  6.4 2.3 %collective-permute-done.2.refs_2_ = bf16[48,1024]{1,0:T(8,128)(2,1)S(1)} collective-permute-done((bf16[48,1024]{1,0:T(8,128)(2,1)}, bf16[48,1024]{1,0:T(8,128)(2,1)S(1)}, u32[]{:S(2)}, u32[]{:S(2)}) %collective-permute-start.2) | collective-permute-done | bytes 98336 | tf_op jit(solution)/shard_map/ppermute | solution.py:43
  8.7 1.2 %collective-permute-done.1.refs_1_ = bf16[48,1024]{1,0:T(8,128)(2,1)S(1)} collective-permute-done((bf16[48,1024]{1,0:T(8,128)(2,1)}, bf16[48,1024]{1,0:T(8,128)(2,1)S(1)}, u32[]{:S(2)}, u32[]{:S(2)}) %collective-permute-start.1) | collective-permute-done | bytes 98336 | tf_op jit(solution)/shard_map/ppermute | solution.py:43
  10.0 0.0 copy-start
  10.0 0.9 %copy-done = bf16[1,48,1024]{2,1,0:T(8,128)(2,1)S(1)} copy-done((bf16[1,48,1024]{2,1,0:T(8,128)(2,1)S(1)}, bf16[1,48,1024]{2,1,0:T(8,128)(2,1)}, u32[]{:S(2)}) %copy-start) | copy-done | bytes 98328
  10.9 0.5 group_bank.1.h0
  11.4 2.3 %collective-permute-start.6 = (bf16[4,48,1024]{2,1,0:T(8,128)(2,1)S(1)}, bf16[4,48,1024]{2,1,0:T(8,128)(2,1)S(1)}, u32[]{:S(2)}, u32[]{:S(2)}) collective-permute-start(bf16[4,48,1024]{2,1,0:T(8,128)(2,1)S(1)} %group_bank.1.h0), channel_id=1, source_target_pairs={{0,24},{1,7},{2,26},{3,1},{4,28},{5,3},{6,30},{7,5},{8,0},{9,15},{... | collective-permute-start | bytes 1179656 | tf_op jit(solution)/shard_map/ppermute | solution.py:43
  13.6 0.5 collective-permute-start.5
  14.2 0.6 collective-permute-start.4
  14.8 2.9 %collective-permute-start = (s32[4]{0:T(128)}, s32[4]{0:T(128)S(1)}, u32[]{:S(2)}, u32[]{:S(2)}) collective-permute-start(s32[4]{0:T(128)} %bitcast.15), channel_id=1, source_target_pairs={{0,1},{1,0},{2,3},{3,2},{4,5},{5,4},{6,7},{7,6},{8,9},{9,8},{10,11... | collective-permute-start | bytes 56 | tf_op jit(solution)/shard_map/ppermute | solution.py:83
  17.6 1.0 %collective-permute-done.their_ids = s32[4]{0:T(128)S(1)} collective-permute-done((s32[4]{0:T(128)}, s32[4]{0:T(128)S(1)}, u32[]{:S(2)}, u32[]{:S(2)}) %collective-permute-start) | collective-permute-done | bytes 48 | tf_op jit(solution)/shard_map/ppermute | solution.py:83
  18.6 4.0 %collective-permute-done.6.h3 = bf16[4,48,1024]{2,1,0:T(8,128)(2,1)S(1)} collective-permute-done((bf16[4,48,1024]{2,1,0:T(8,128)(2,1)S(1)}, bf16[4,48,1024]{2,1,0:T(8,128)(2,1)S(1)}, u32[]{:S(2)}, u32[]{:S(2)}) %collective-permute-start.6) | collective-permute-done | bytes 393248 | tf_op jit(solution)/shard_map/ppermute | solution.py:43
  22.6 0.0 collective-permute-done.5.h2
  22.6 3.7 %collective-permute-done.4.h1 = bf16[4,48,1024]{2,1,0:T(8,128)(2,1)S(1)} collective-permute-done((bf16[4,48,1024]{2,1,0:T(8,128)(2,1)S(1)}, bf16[4,48,1024]{2,1,0:T(8,128)(2,1)S(1)}, u32[]{:S(2)}, u32[]{:S(2)}) %collective-permute-start.4) | collective-permute-done | bytes 393248 | tf_op jit(solution)/shard_map/ppermute | solution.py:43
  26.3 0.9 %select.1 = bf16[4,48,1024]{2,1,0:T(8,128)(2,1)S(1)} custom-call(s32[4]{0:T(128)S(1)} %collective-permute-done.their_ids, bf16[4,48,1024]{2,1,0:T(8,128)(2,1)S(1)} %group_bank.1.h0, bf16[4,48,1024]{2,1,0:T(8,128)(2,1)S(1)} %collective-permute-done.4.h1, bf16[4,48,1024]{2,1,0:T(8,128)(2,1)S(1)} %collective-permute-done.5.h2, ...), custom_call_target="tpu_custom_call" | custom-call | tf_op jit(solution)/shard_map/select/pallas_call | solution.py:431
  27.2 3.3 %collective-permute-start.7 = (bf16[4,48,1024]{2,1,0:T(8,128)(2,1)S(1)}, bf16[4,48,1024]{2,1,0:T(8,128)(2,1)S(1)}, u32[]{:S(2)}, u32[]{:S(2)}) collective-permute-start(bf16[4,48,1024]{2,1,0:T(8,128)(2,1)S(1)} %select.1), channel_id=1, source_target_pairs={{0,1},{1,0},{2,3},{3,2},{4,5},{5,4},{6,7},{7,6},{8,9},{9,8},{10,11... | collective-permute-start | bytes 1179656 | tf_op jit(solution)/shard_map/ppermute | solution.py:83
  30.5 1.5 %broadcast_in_dim.3 = f32[32,2,1024]{2,1,0:T(2,128)} broadcast(f32[2,1024]{1,0:T(2,128)} %bitcast.19), dimensions={1,2} | broadcast | bytes 270336 | tf_op jit(solution)/shard_map/broadcast_in_dim | solution.py:29
  32.0 0.0 copy-start.1
  32.0 0.0 copy-start.3
  32.0 3.8 %all-to-all-start = ((f32[32,2,1024]{2,1,0:T(2,128)}), f32[32,2,1024]{2,1,0:T(2,128)S(1)}, u32[]{:S(2)}, u32[]{:S(2)}) async-start(f32[32,2,1024]{2,1,0:T(2,128)} %broadcast_in_dim.3), calls=%async_computation | async-start | bytes 524288 | tf_op jit(solution)/shard_map/all_to_all | solution.py:30
  37.1 7.6 %all-to-all-done.rows = f32[32,2,1024]{2,1,0:T(2,128)S(1)} async-done(((f32[32,2,1024]{2,1,0:T(2,128)}), f32[32,2,1024]{2,1,0:T(2,128)S(1)}, u32[]{:S(2)}, u32[]{:S(2)}) %all-to-all-start) | async-done | bytes 262176 | tf_op jit(solution)/shard_map/all_to_all | solution.py:30
  44.6 0.0 copy-start.2
  44.6 0.7 copy-done.2
  45.3 13.2 %covariance.1 = (bf16[4,1024,1024]{2,1,0:T(8,128)(2,1)}, f32[4,8,128]{2,1,0:T(8,128)S(1)}, f32[256,1,128]{2,1,0:T(1,128)}) custom-call(s32[1]{0:T(128)S(6)} %copy.13.order, f32[1]{0:T(128)S(6)} %copy.12.reach, s32[4]{0:T(128)S(1)} %bitcast.17, f32[32,2,1024]{2,1,0:T(2,128)S(1)} %all-to-all-done.rows), custom_call_target="tpu_custom_call" | custom-call | flops 100000000 | bytes 8388608 | tf_op jit(solution)/shard_map/covariance/pallas_call | solution.py:362
  58.5 9.5 %all-to-all-start.1 = ((f32[256,1,128]{2,1,0:T(1,128)}), f32[256,1,128]{2,1,0:T(1,128)S(1)}, u32[]{:S(2)}, u32[]{:S(2)}) async-start(f32[256,1,128]{2,1,0:T(1,128)} %get-tuple-element.16), calls=%async_computation.1 | async-start | bytes 262144 | tf_op jit(solution)/shard_map/all_to_all | solution.py:441
  68.0 0.0 collective-permute-done.7.got
  68.0 0.0 copy-done.1
  68.0 0.0 copy-done.3
  68.0 16.8 %compress.1 = (f32[4,48,1024]{2,1,0:T(8,128)}, f32[4,48,1024]{2,1,0:T(8,128)}, f32[4,8,128]{2,1,0:T(8,128)S(1)}) custom-call(s32[4]{0:T(128)S(1)} %bitcast.16, s32[4]{0:T(128)S(1)} %bitcast.18, f32[4,8,128]{2,1,0:T(8,128)S(1)} %get-tuple-element.12.norms, bf16[4,1024,1024]{2,1,0:T(8,128)(2,1)} %get-tuple-element.13.low_hbm, ...), custom_call_target="tpu_custom_call" | custom-call | flops 2000000000 | bytes 8388608 | tf_op jit(solution)/shard_map/compress/pallas_call | solution.py:391
  84.8 0.0 all-to-all-done.1.total
  84.8 0.9 %errors.1 = (f32[1,4]{1,0:T(1,128)}, s32[1]{0:T(128)}) custom-call(f32[256,1,128]{2,1,0:T(1,128)S(1)} %all-to-all-done.1.total, f32[4,8,128]{2,1,0:T(8,128)S(1)} %get-tuple-element.17.errs), custom_call_target="tpu_custom_call" | custom-call | tf_op jit(solution)/shard_map/errors/pallas_call | solution.py:445
Async XLA Ops:
  0.6 5.8 %collective-permute-start.3 = (bf16[48,1024]{1,0:T(8,128)(2,1)}, bf16[48,1024]{1,0:T(8,128)(2,1)S(1)}, u32[]{:S(2)}, u32[]{:S(2)}) collective-permute-start(bf16[48,1024]{1,0:T(8,128)(2,1)} %bitcast.11), channel_id=1, source_target_pairs={{0,6},{1,25},{2,0},{3,27},{4,2},{5,29},{6,4},{7,31},{8,14},{9,1},{... | collective-permute-start | bytes 294920 | tf_op jit(solution)/shard_map/ppermute | solution.py:43
  3.4 5.3 %collective-permute-start.2 = (bf16[48,1024]{1,0:T(8,128)(2,1)}, bf16[48,1024]{1,0:T(8,128)(2,1)S(1)}, u32[]{:S(2)}, u32[]{:S(2)}) collective-permute-start(bf16[48,1024]{1,0:T(8,128)(2,1)} %bitcast.12), channel_id=1, source_target_pairs={{0,4},{1,17},{2,6},{3,19},{4,0},{5,21},{6,2},{7,23},{8,12},{9,25},... | collective-permute-start | bytes 294920 | tf_op jit(solution)/shard_map/ppermute | solution.py:43
  3.8 6.2 %collective-permute-start.1 = (bf16[48,1024]{1,0:T(8,128)(2,1)}, bf16[48,1024]{1,0:T(8,128)(2,1)S(1)}, u32[]{:S(2)}, u32[]{:S(2)}) collective-permute-start(bf16[48,1024]{1,0:T(8,128)(2,1)} %bitcast.13), channel_id=1, source_target_pairs={{0,2},{1,9},{2,4},{3,11},{4,6},{5,13},{6,0},{7,15},{8,10},{9,17},{... | collective-permute-start | bytes 294920 | tf_op jit(solution)/shard_map/ppermute | solution.py:43
  10.0 0.9 %copy-start = (bf16[1,48,1024]{2,1,0:T(8,128)(2,1)S(1)}, bf16[1,48,1024]{2,1,0:T(8,128)(2,1)}, u32[]{:S(2)}) copy-start(bf16[1,48,1024]{2,1,0:T(8,128)(2,1)} %param.9) | copy-start | bytes 294916
  11.4 11.2 %collective-permute-start.6 = (bf16[4,48,1024]{2,1,0:T(8,128)(2,1)S(1)}, bf16[4,48,1024]{2,1,0:T(8,128)(2,1)S(1)}, u32[]{:S(2)}, u32[]{:S(2)}) collective-permute-start(bf16[4,48,1024]{2,1,0:T(8,128)(2,1)S(1)} %group_bank.1.h0), channel_id=1, source_target_pairs={{0,24},{1,7},{2,26},{3,1},{4,28},{5,3},{6,30},{7,5},{8,0},{9,15},{... | collective-permute-start | bytes 1179656 | tf_op jit(solution)/shard_map/ppermute | solution.py:43
  13.6 8.9 %collective-permute-start.5 = (bf16[4,48,1024]{2,1,0:T(8,128)(2,1)S(1)}, bf16[4,48,1024]{2,1,0:T(8,128)(2,1)S(1)}, u32[]{:S(2)}, u32[]{:S(2)}) collective-permute-start(bf16[4,48,1024]{2,1,0:T(8,128)(2,1)S(1)} %group_bank.1.h0), channel_id=1, source_target_pairs={{0,16},{1,5},{2,18},{3,7},{4,20},{5,1},{6,22},{7,3},{8,24},{9,13},... | collective-permute-start | bytes 1179656 | tf_op jit(solution)/shard_map/ppermute | solution.py:43
  14.2 12.1 %collective-permute-start.4 = (bf16[4,48,1024]{2,1,0:T(8,128)(2,1)S(1)}, bf16[4,48,1024]{2,1,0:T(8,128)(2,1)S(1)}, u32[]{:S(2)}, u32[]{:S(2)}) collective-permute-start(bf16[4,48,1024]{2,1,0:T(8,128)(2,1)S(1)} %group_bank.1.h0), channel_id=1, source_target_pairs={{0,8},{1,3},{2,10},{3,5},{4,12},{5,7},{6,14},{7,1},{8,16},{9,11},{... | collective-permute-start | bytes 1179656 | tf_op jit(solution)/shard_map/ppermute | solution.py:43
  14.8 3.8 %collective-permute-start = (s32[4]{0:T(128)}, s32[4]{0:T(128)S(1)}, u32[]{:S(2)}, u32[]{:S(2)}) collective-permute-start(s32[4]{0:T(128)} %bitcast.15), channel_id=1, source_target_pairs={{0,1},{1,0},{2,3},{3,2},{4,5},{5,4},{6,7},{7,6},{8,9},{9,8},{10,11... | collective-permute-start | bytes 56 | tf_op jit(solution)/shard_map/ppermute | solution.py:83
  27.2 40.8 %collective-permute-start.7 = (bf16[4,48,1024]{2,1,0:T(8,128)(2,1)S(1)}, bf16[4,48,1024]{2,1,0:T(8,128)(2,1)S(1)}, u32[]{:S(2)}, u32[]{:S(2)}) collective-permute-start(bf16[4,48,1024]{2,1,0:T(8,128)(2,1)S(1)} %select.1), channel_id=1, source_target_pairs={{0,1},{1,0},{2,3},{3,2},{4,5},{5,4},{6,7},{7,6},{8,9},{9,8},{10,11... | collective-permute-start | bytes 1179656 | tf_op jit(solution)/shard_map/ppermute | solution.py:83
  32.0 36.1 %copy-start.1 = (s32[4,1,1,1]{0,3,2,1:T(1,128)S(1)}, s32[4,1,1,1]{0,3,2,1:T(1,128)}, u32[]{:S(2)}) copy-start(s32[4,1,1,1]{0,3,2,1:T(1,128)} %param.10) | copy-start | bytes 52
  32.0 36.1 %copy-start.3 = (s32[4,1,1,1]{0,3,2,1:T(1,128)S(1)}, s32[4,1,1,1]{0,3,2,1:T(1,128)}, u32[]{:S(2)}) copy-start(s32[4,1,1,1]{0,3,2,1:T(1,128)} %param.11) | copy-start | bytes 52
  32.0 12.7 %all-to-all-start = ((f32[32,2,1024]{2,1,0:T(2,128)}), f32[32,2,1024]{2,1,0:T(2,128)S(1)}, u32[]{:S(2)}, u32[]{:S(2)}) async-start(f32[32,2,1024]{2,1,0:T(2,128)} %broadcast_in_dim.3), calls=%async_computation | async-start | bytes 524288 | tf_op jit(solution)/shard_map/all_to_all | solution.py:30
  44.6 0.7 copy-start.2
  58.5 26.3 %all-to-all-start.1 = ((f32[256,1,128]{2,1,0:T(1,128)}), f32[256,1,128]{2,1,0:T(1,128)S(1)}, u32[]{:S(2)}, u32[]{:S(2)}) async-start(f32[256,1,128]{2,1,0:T(1,128)} %get-tuple-element.16), calls=%async_computation.1 | async-start | bytes 262144 | tf_op jit(solution)/shard_map/all_to_all | solution.py:441
